TPU v7x, 32 devices: a whole 2x2x4 slice. The times are simulated.
32 devices in a mesh: seq: 4 (over y, x), batch: 8 (over z, core).
Axes of the slice: x: 2, y: 2, z: 4, core: 2. Of those that a mesh axis runs over, the one named last changes fastest.
Arguments:
- activations: bfloat16 [8, 3072, 4096], P('batch', 'seq'), may hold values from -18 to 18
- out_grads: bfloat16 [8, 3072, 4096], P('batch', 'seq'), may hold values from -0.29882812 to 0.29882812
- lengths: int32 [8, 3], P('batch'), may hold values from 1 to 1536, 3072 in all within a row
Outputs:
- act_factor: float32 [4096, 4096], P(('seq', 'batch'))
- grad_factor: float32 [4096, 4096], P(('seq', 'batch'))
Inputs may be any that keep to these rules, and one draw needn't show every extreme that they name: `lengths`: each row sums to 3072 and its largest entry is exactly 1536.
All inputs are finite; a program needn't handle non-finite values.
Results may differ from a plain program's by a relative error of at most 0.004.
Values may be sent and summed in bfloat16 or wider, within the bound.
No kernel may reach another device: no remote copies, remote signals or barrier semaphores. Data moves between devices by JAX's collectives and lax.ppermute only.
A program may use at most 64 MiB of HBM per device.

v0:
```python
import jax
import jax.numpy as jnp
from jax import lax
from jax.sharding import PartitionSpec as P


def local(activations, out_grads, lengths):
    act_local = activations[0]
    grad_local = out_grads[0]
    seq_lengths = lengths[0]
    tok_count = act_local.shape[0]
    width = act_local.shape[1]
    seq_count = seq_lengths.shape[0]
    group_size = lax.axis_size("seq")
    devices = group_size * lax.axis_size("batch")
    tile_rows = width // devices
    tile_start = lax.axis_index(("seq", "batch")) * tile_rows
    total_seqs = seq_count * lax.axis_size("batch")
    ends = jnp.cumsum(seq_lengths)
    starts = ends - seq_lengths
    position = lax.axis_index("seq") * tok_count + jnp.arange(tok_count, dtype=jnp.int32)
    member = (position[None, :] >= starts[:, None]) & (position[None, :] < ends[:, None])
    member = member.astype(jnp.bfloat16)
    act_part = jnp.dot(member, act_local, preferred_element_type=jnp.float32)
    grad_part = jnp.dot(member, grad_local, preferred_element_type=jnp.float32)
    act_sum, grad_sum = lax.psum((act_part, grad_part), "seq")
    act_rows = (act_sum / seq_lengths[:, None].astype(jnp.float32)).astype(jnp.bfloat16)
    grad_rows = grad_sum.astype(jnp.bfloat16)
    act_piece = lax.all_gather(act_rows, "batch", axis=0, tiled=True)
    grad_piece = lax.all_gather(grad_rows, "batch", axis=0, tiled=True)
    act_cols = lax.dynamic_slice_in_dim(act_piece, tile_start, tile_rows, 1)
    grad_cols = lax.dynamic_slice_in_dim(grad_piece, tile_start, tile_rows, 1)
    dims = (((0,), (0,)), ((), ()))
    act_new = lax.dot_general(act_cols, act_piece, dims, preferred_element_type=jnp.float32)
    grad_new = lax.dot_general(grad_cols, grad_piece, dims, preferred_element_type=jnp.float32)
    return (act_new / total_seqs, grad_new / total_seqs)


def solution(mesh):
    in_specs = (P("batch", "seq", None), P("batch", "seq", None), P("batch", None))
    out_specs = (P(("seq", "batch"), None), P(("seq", "batch"), None))
    return jax.shard_map(local, mesh=mesh, in_specs=in_specs, out_specs=out_specs, check_vma=False)
```

profile of v0, /device:TPU:0, one launch (start us, length us, event | category | flops | bytes accessed | tf_op | source)
XLA Modules:
  0.0 60.4 jit_solution(18398643600127713620)
XLA Ops:
  0.6 0.8 %reduce-window.7 = s32[3,1]{0,1:T(1,128)S(1)} reduce-window(s32[3,1]{0,1:T(1,128)} %bitcast.22, s32[]{:T(128)} %constant.7.clone.1), window={size=3x1 pad=2_0x0_0}, to_apply=%region_0.0 | reduce-window | flops 6 | bytes 28 | tf_op jit(solution)/shard_map/reduce-window.2
  1.5 0.0 copy-start
  1.5 0.8 %bitcast_subtract_fusion = s32[3]{0:T(128)S(1)} fusion(s32[1,3]{1,0:T(1,128)} %param.5, s32[3,1]{0,1:T(1,128)S(1)} %reduce-window.7), kind=kLoop, calls=%fused_computation.14 | loop fusion | flops 3 | bytes 36 | tf_op jit(solution)/shard_map/sub | solution.py:20
  2.3 0.8 %bitcast_convert_fusion = f32[3]{0:T(128)S(1)} fusion(s32[1,3]{1,0:T(1,128)} %param.5), kind=kLoop, calls=%fused_computation.13 | loop fusion | flops 3 | bytes 24 | tf_op jit(solution)/shard_map/convert_element_type | solution.py:27
  3.1 4.0 %fusion = f32[3,4096]{1,0:T(4,128)S(1)} fusion(bf16[1,768,4096]{2,1,0:T(8,128)(2,1)} %param.4, s32[768]{0:T(1024)S(1)} %iota_add_fusion, s32[3]{0:T(128)S(1)} %bitcast.20, s32[3]{0:T(128)S(1)} %bitcast_subtract_fusion), kind=kOutput, calls=%fused_computation | convolution fusion | flops 18881280 | bytes 6343704 | tf_op jit(solution)/shard_map/dot_general | solution.py:25
  7.1 0.0 copy-done
  7.1 1.0 %fusion.2 = f32[3,4096]{1,0:T(4,128)S(1)} fusion(bf16[1,768,4096]{2,1,0:T(8,128)(2,1)S(1)} %copy-done, s32[768]{0:T(1024)S(1)} %iota_add_fusion, s32[3]{0:T(128)S(1)} %bitcast.21, s32[3]{0:T(128)S(1)} %bitcast_subtract_fusion), kind=kOutput, calls=%fused_computation.2 | convolution fusion | flops 18881280 | bytes 6343704 | tf_op jit(solution)/shard_map/dot_general | solution.py:24
  8.0 19.8 %all-reduce.2 = (f32[3,4096]{1,0:T(4,128)S(1)}, bf16[3,4096]{1,0:T(4,128)(2,1)S(1)}) all-reduce(f32[3,4096]{1,0:T(4,128)S(1)} %fusion.2, f32[3,4096]{1,0:T(4,128)S(1)} %fusion), channel_id=1, replica_groups=mesh['seq'=4,'batch'=8] {'seq'}, use_global_device_ids=true, to_apply=%region_1.2 | all-reduce | flops 24576 | bytes 172032 | tf_op jit(solution)/shard_map/psum | solution.py:26
  27.8 0.1 fusion.4
  27.9 14.4 %all-gather.1 = bf16[8,3,4096]{2,1,0:T(4,128)(2,1)S(1)} all-gather(bf16[1,3,4096]{2,1,0:T(4,128)(2,1)S(1)} %bitcast.19), channel_id=1, replica_groups=mesh['seq'=4,'batch'=8] {'batch'}, dimensions={0}, use_global_device_ids=true | all-gather | bytes 221184 | tf_op jit(solution)/shard_map/all_gather | solution.py:30
  42.3 0.2 reshape.48
  42.5 14.2 %all-gather = bf16[8,3,4096]{2,1,0:T(4,128)(2,1)S(1)} all-gather(bf16[1,3,4096]{2,1,0:T(4,128)(2,1)S(1)} %fusion.4), channel_id=1, replica_groups=mesh['seq'=4,'batch'=8] {'batch'}, dimensions={0}, use_global_device_ids=true | all-gather | bytes 221184 | tf_op jit(solution)/shard_map/all_gather | solution.py:29
  56.7 0.2 reshape.46
  56.9 1.8 %convolution_multiply_fusion.1 = f32[128,4096]{1,0:T(8,128)} fusion(bf16[24,4096]{1,0:T(8,128)(2,1)S(1)} %reshape.46, s32[]{:T(128)S(6)} %select_n.4), kind=kOutput, calls=%fused_computation.5 | convolution fusion | flops 25690112 | bytes 2299908 | tf_op jit(solution)/shard_map/dot_general | solution.py:34
  58.7 1.8 %convolution_multiply_fusion = f32[128,4096]{1,0:T(8,128)} fusion(bf16[24,4096]{1,0:T(8,128)(2,1)S(1)} %reshape.48, s32[]{:T(128)S(6)} %select_n.4), kind=kOutput, calls=%fused_computation.4 | convolution fusion | flops 25690112 | bytes 2299908 | tf_op jit(solution)/shard_map/dot_general | solution.py:35
  (1 shorter events, 0.0 us)
Async XLA Ops:
  1.5 5.6 %copy-start = (bf16[1,768,4096]{2,1,0:T(8,128)(2,1)S(1)}, bf16[1,768,4096]{2,1,0:T(8,128)(2,1)}, u32[]{:S(2)}) copy-start(bf16[1,768,4096]{2,1,0:T(8,128)(2,1)} %param.3) | copy-start | bytes 18874372
where the time goes:
time: 60.7 us; the launch traced here: 60.4 us
  blocking collectives  48.4 us (80%)
  matrix products  8.53 us (14%)
  other arithmetic  2.51 us (4%)
  between operations  0.67 us (1%)
    psum x1, blocking collectives, local(): act_sum, grad_sum = lax.psum((act_part, grad_part), 'seq')  19.8 us
    all_gather x1, blocking collectives, local(): grad_piece = lax.all_gather(grad_rows, 'batch', axis=0, tiled=True)  14.4 us
    all_gather x1, blocking collectives, local(): act_piece = lax.all_gather(act_rows, 'batch', axis=0, tiled=True)  14.2 us
    dot_general x1, matrix products, local(): grad_part = jnp.dot(member, grad_local, preferred_element_type=jnp.float32)  3.99 us
    dot_general x1, matrix products, local(): lax.dot_general(act_cols, act_piece, dims, preferred_element_type=jnp.flo...  1.79 us
    dot_general x1, matrix products, local(): lax.dot_general(grad_cols, grad_piece, dims, preferred_element_type=jnp.f...  1.78 us

commit v1 on v0

v1 whole, which is shorter than its diff:
```python
import functools

import jax
import jax.numpy as jnp
from jax import lax
from jax.experimental import pallas as pl
from jax.experimental.pallas import tpu as pltpu
from jax.sharding import Mesh
from jax.sharding import PartitionSpec as P

LANES = 128
ROWS = 8


def spare_split(rows, width):
    spare = ROWS - rows
    if spare <= 0 or rows % spare or (width * rows) % (ROWS * LANES):
        return width, 0
    kept = width * rows // ROWS
    tail = width - kept
    if tail % LANES:
        return width, 0
    return kept, tail


def peers(count):
    return list(range(count - 1, -1, -1))


def partner(index, offset, count):
    if count & (count - 1) == 0:
        return index ^ offset
    return (index + offset) % count


def segment_kernel(seq_count, chunk_count, slabs, act, grad, lens, *refs):
    outs = refs[:chunk_count]
    act_buf, grad_buf, len_buf, act_sem, grad_sem, len_sem = refs[chunk_count:]
    tokens = act.shape[1]
    slab = act_buf.shape[2]
    width = outs[0].shape[1]
    me = lax.axis_index("seq")
    len_copy = pltpu.make_async_copy(lens, len_buf, len_sem)
    len_copy.start()
    copies = []
    for slot, offset in enumerate(peers(chunk_count)):
        base = partner(me, offset, chunk_count) * width
        for part in range(slabs):
            at = slot * slabs + part
            cols = pl.ds(pl.multiple_of(base + part * slab, slab), slab)
            pair = (
                pltpu.make_async_copy(act.at[0, :, cols], act_buf.at[at], act_sem.at[at]),
                pltpu.make_async_copy(grad.at[0, :, cols], grad_buf.at[at], grad_sem.at[at]),
            )
            for copy in pair:
                copy.start()
            copies.append(pair)
    len_copy.wait()
    row = lax.broadcasted_iota(jnp.int32, (ROWS, tokens), 0)
    position = lax.broadcasted_iota(jnp.int32, (ROWS, tokens), 1) + me * tokens
    low = jnp.zeros((ROWS, tokens), jnp.int32)
    high = jnp.zeros((ROWS, tokens), jnp.int32)
    start = jnp.int32(0)
    for s in range(seq_count):
        end = start + len_buf[0, s]
        mine = (row == s) | (row == s + seq_count)
        low = jnp.where(mine, start, low)
        high = jnp.where(mine, end, high)
        start = end
    member = (position >= low) & (position < high)
    act_member = jnp.where(member & (row < seq_count), 1.0, 0.0).astype(jnp.bfloat16)
    grad_member = jnp.where(member & (row >= seq_count), 1.0, 0.0).astype(jnp.bfloat16)
    for slot, offset in enumerate(peers(chunk_count)):
        for part in range(slabs):
            at = slot * slabs + part
            for copy in copies[at]:
                copy.wait()
            sums = jnp.dot(act_member, act_buf[at], preferred_element_type=jnp.float32)
            sums += jnp.dot(grad_member, grad_buf[at], preferred_element_type=jnp.float32)
            outs[offset][:, part * slab : (part + 1) * slab] = sums


def rows_kernel(seq_count, kept, tail, lens, *refs):
    parts, out = refs[:-1], refs[-1]
    total = parts[0][...]
    for part in parts[1:]:
        total += part[...]
    rows = 2 * seq_count
    row = lax.broadcasted_iota(jnp.int32, (ROWS, 1), 0)
    count = jnp.ones((ROWS, 1), jnp.float32)
    for s in range(seq_count):
        count = jnp.where(row == s, lens[0, s].astype(jnp.float32), count)
    total = total / count
    if tail:
        spare = ROWS - rows
        per = rows // spare
        body = total[:, :kept]
        pieces = []
        for k in range(per):
            piece = jnp.zeros((ROWS, tail), jnp.float32)
            for j in range(spare):
                source = total[j * per + k : j * per + k + 1, kept:]
                piece = jnp.where(row == rows + j, source, piece)
            pieces.append(piece)
        packed = jnp.where(row >= rows, jnp.concatenate(pieces, axis=1), body)
    else:
        packed = total
    packed = packed.astype(jnp.bfloat16)
    for g in range(out.shape[0]):
        out[g] = packed


def factor_kernel(seq_count, total_seqs, kept, tail, near, far, act_out, grad_out, stack):
    chunks, pairs = near.shape[0], near.shape[1]
    rows = 2 * seq_count
    width = kept + tail
    half = pairs * ROWS
    row = lax.broadcasted_iota(jnp.int32, (1, ROWS, 1), 1)
    for side, ref in enumerate((near, far)):
        for c in range(chunks):
            block = ref[c]
            at = slice(side * half, (side + 1) * half)
            stack[at, c * width : c * width + kept] = block.reshape(half, kept)
            if tail:
                spare = ROWS - rows
                per = rows // spare
                wide = block.astype(jnp.float32)
                rest = jnp.zeros((pairs, ROWS, tail), jnp.float32)
                for j in range(spare):
                    for k in range(per):
                        source = wide[:, rows + j : rows + j + 1, k * tail : (k + 1) * tail]
                        rest = jnp.where(row == j * per + k, source, rest)
                stack[at, c * width + kept : (c + 1) * width] = rest.astype(jnp.bfloat16).reshape(half, tail)
    tile = act_out.shape[0]
    span = max(tile, LANES)
    me = (lax.axis_index("seq") * lax.axis_size("pair") + lax.axis_index("pair")) * lax.axis_size("core") + lax.axis_index("core")
    first = me * tile
    base = pl.multiple_of(first // LANES * LANES, LANES)
    left = stack[:, pl.ds(base, span)].astype(jnp.float32)
    if tile < span:
        left = pltpu.roll(left, span - (first - base), 1)
    kind = lax.rem(lax.broadcasted_iota(jnp.int32, left.shape, 0), ROWS)
    act_left = jnp.where(kind < seq_count, left, 0.0).astype(jnp.bfloat16)
    grad_left = jnp.where((kind >= seq_count) & (kind < rows), left, 0.0).astype(jnp.bfloat16)
    dims = (((0,), (0,)), ((), ()))
    for out, lhs in ((act_out, act_left), (grad_out, grad_left)):
        product = lax.dot_general(lhs[:, :tile], stack[...], dims, preferred_element_type=jnp.float32)
        out[...] = product * (1.0 / total_seqs)


def local(activations, out_grads, lengths):
    chunks = lax.axis_size("seq")
    pairs = lax.axis_size("pair")
    cores = lax.axis_size("core")
    tokens, depth = activations.shape[1], activations.shape[2]
    seq_count = lengths.shape[1]
    width = depth // chunks
    slabs = 2 if width % (2 * LANES) == 0 else 1
    slab = width // slabs
    devices = chunks * pairs * cores
    tile = depth // devices
    kept, tail = spare_split(2 * seq_count, width)
    vmem = pl.BlockSpec(memory_space=pltpu.VMEM)
    anywhere = pl.BlockSpec(memory_space=pl.ANY)

    parts = pl.pallas_call(
        functools.partial(segment_kernel, seq_count, chunks, slabs),
        out_shape=[jax.ShapeDtypeStruct((ROWS, width), jnp.float32)] * chunks,
        in_specs=[anywhere] * 3,
        out_specs=[vmem] * chunks,
        scratch_shapes=[
            pltpu.VMEM((chunks * slabs, tokens, slab), jnp.bfloat16),
            pltpu.VMEM((chunks * slabs, tokens, slab), jnp.bfloat16),
            pltpu.SMEM(lengths.shape, jnp.int32),
            pltpu.SemaphoreType.DMA((chunks * slabs,)),
            pltpu.SemaphoreType.DMA((chunks * slabs,)),
            pltpu.SemaphoreType.DMA,
        ],
        name="segment_sums",
    )(activations, out_grads, lengths)

    arrived = [parts[0]]
    for offset in peers(chunks)[:-1]:
        ring = [(i, partner(i, offset, chunks)) for i in range(chunks)]
        arrived.append(lax.ppermute(parts[offset], "seq", ring))

    spread = pl.pallas_call(
        functools.partial(rows_kernel, seq_count, kept, tail),
        out_shape=jax.ShapeDtypeStruct((chunks * pairs, ROWS, kept), jnp.bfloat16),
        in_specs=[pl.BlockSpec(memory_space=pltpu.SMEM)] + [vmem] * chunks,
        out_specs=vmem,
        name="mean_rows",
    )(lengths, *arrived)

    near = lax.all_to_all(spread, ("seq", "pair"), 0, 0, tiled=True)
    far = lax.ppermute(near, "core", [(i, (i + 1) % cores) for i in range(cores)])
    near, far = (a.reshape(chunks, pairs, ROWS, kept) for a in (near, far))

    return pl.pallas_call(
        functools.partial(factor_kernel, seq_count, seq_count * pairs * cores, kept, tail),
        out_shape=[jax.ShapeDtypeStruct((tile, depth), jnp.float32)] * 2,
        in_specs=[vmem] * 2,
        out_specs=[vmem] * 2,
        scratch_shapes=[pltpu.VMEM((2 * pairs * ROWS, depth), jnp.bfloat16)],
        name="factor_tiles",
    )(near, far)


def solution(mesh):
    batch = mesh.shape["batch"]
    split = Mesh(mesh.devices.reshape(mesh.shape["seq"], batch // 2, 2), ("seq", "pair", "core"))
    groups = ("pair", "core")
    in_specs = (P(groups, "seq", None), P(groups, "seq", None), P(groups, None))
    out_specs = (P(("seq",) + groups, None), P(("seq",) + groups, None))

    def program(activations, out_grads, lengths):
        return tuple(jax.shard_map(local, mesh=split, in_specs=in_specs, out_specs=out_specs, check_vma=False)(activations, out_grads, lengths))

    return program
```

time: 60.7 us -> 37.2 us (0.61)
  blocking collectives: 48.4 us -> 14 us
  Pallas kernels: 0 us -> 10.9 us
  matrix products: 8.53 us -> 0 us
  waiting for transfers between devices: 0 us -> 5.42 us
  starting transfers between devices: 0 us -> 4.63 us
  other arithmetic: 2.51 us -> 0 us
  local copies, waits for them, and re-layouts: 0.34 us -> 1.27 us
    all_gather x2 -> x0, blocking collectives: 28.6 us -> none  [the longest x1 14.4 us: local(): grad_piece = lax.all_gather(grad_rows, 'batch', axis=0, tiled=True)]
    psum x1 -> x0, blocking collectives: 19.8 us -> none  [local(): act_sum, grad_sum = lax.psum((act_part, grad_part), 'seq')]
    all_to_all x0 -> x1, blocking collectives: none -> 14 us  [local(): near = lax.all_to_all(spread, ('seq', 'pair'), 0, 0, tiled=True)]
    pallas_call x0 -> x3, Pallas kernels: none -> 10.9 us  [the longest x1 5.78 us: local(): pl.pallas_call(functools.partial(segment_kernel, seq_count, chunks, slabs...]
    dot_general x4 -> x0, matrix products: 8.53 us -> none  [the longest x1 3.99 us: local(): grad_part = jnp.dot(member, grad_local, preferred_element_type=jnp.float32)]
    ppermute x0 -> x4, waiting for transfers between devices: none -> 5.42 us  [the longest x3 3.98 us: local(): arrived.append(lax.ppermute(parts[offset], 'seq', ring))]
    ppermute x0 -> x4, starting transfers between devices: none -> 4.63 us  [the longest x3 4.63 us: local(): arrived.append(lax.ppermute(parts[offset], 'seq', ring))]
    unnamed x4 -> x10, local copies, waits for them, and re-layouts: 0.34 us -> 1.27 us
  transfers between devices with their start and end apart: 0 -> 4, of which waited for: 0 -> 4; matrix products, arithmetic and copies ran while one was open for 0% -> 0% of each run, Pallas kernels for 0% -> 0%
where the time goes in v1:
time: 37.2 us; the launch traced here: 36.9 us
  blocking collectives  14 us (38%)
  Pallas kernels  10.9 us (29%)
  waiting for transfers between devices  5.42 us (15%)
  starting transfers between devices  4.63 us (12%)
  local copies, waits for them, and re-layouts  1.27 us (3%)
  between operations  0.65 us (2%)
    all_to_all x1, blocking collectives, local(): near = lax.all_to_all(spread, ('seq', 'pair'), 0, 0, tiled=True)  14 us
    pallas_call x1, Pallas kernels, local(): pl.pallas_call(functools.partial(segment_kernel, seq_count, chunks, slabs...  5.78 us
    ppermute x3, starting transfers between devices, local(): arrived.append(lax.ppermute(parts[offset], 'seq', ring))  4.63 us
    ppermute x3, waiting for transfers between devices, local(): arrived.append(lax.ppermute(parts[offset], 'seq', ring))  3.98 us
    pallas_call x1, Pallas kernels, local(): pl.pallas_call(functools.partial(factor_kernel, seq_count, seq_count * pa...  3.64 us
    pallas_call x1, Pallas kernels, local(): pl.pallas_call(functools.partial(rows_kernel, seq_count, kept, tail), out...  1.52 us
    ppermute x1, waiting for transfers between devices, local(): lax.ppermute(near, 'core', [(i, (i + 1) % cores) for i in range(cores)])  1.44 us
    unnamed x10, local copies, waits for them, and re-layouts  1.27 us
  transfers between devices with their start and end apart: 4, of which 4 were waited for; matrix products, arithmetic and copies ran while one was open for 0% of the time, Pallas kernels for 0%

profile of v1, /device:TPU:0, one launch (start us, length us, event | category | flops | bytes accessed | tf_op | source)
XLA Modules:
  0.0 36.9 jit_solution(12002036318696143439)
XLA Ops:
  0.6 5.8 %segment_sums.1 = (f32[8,1024]{1,0:T(8,128)}, f32[8,1024]{1,0:T(8,128)}, f32[8,1024]{1,0:T(8,128)}, f32[8,1024]{1,0:T(8,128)}) custom-call(bf16[1,768,4096]{2,1,0:T(8,128)(2,1)} %act.1, bf16[1,768,4096]{2,1,0:T(8,128)(2,1)} %grad.1, s32[1,3]{1,0:T(1,128)} %lens.3), custom_call_target="tpu_custom_call" | custom-call | tf_op jit(solution)/shard_map/segment_sums/pallas_call | solution.py:166
  6.4 4.0 %collective-permute-start = (f32[8,1024]{1,0:T(8,128)}, f32[8,1024]{1,0:T(8,128)S(1)}, u32[]{:S(2)}, u32[]{:S(2)}) collective-permute-start(f32[8,1024]{1,0:T(8,128)} %get-tuple-element.7), channel_id=1, source_target_pairs={{0,24},{8,16},{16,8},{24,0},{1,25},{9,17},{17,9},{25,1},{2,26},{10... | collective-permute-start | bytes 98312 | tf_op jit(solution)/shard_map/ppermute | solution.py:185
  10.4 0.5 %collective-permute-start.1 = (f32[8,1024]{1,0:T(8,128)}, f32[8,1024]{1,0:T(8,128)S(1)}, u32[]{:S(2)}, u32[]{:S(2)}) collective-permute-start(f32[8,1024]{1,0:T(8,128)} %get-tuple-element.8), channel_id=1, source_target_pairs={{0,16},{8,24},{16,0},{24,8},{1,17},{9,25},{17,1},{25,9},{2,18},{10... | collective-permute-start | bytes 98312 | tf_op jit(solution)/shard_map/ppermute | solution.py:185
  10.9 0.1 collective-permute-start.2
  11.0 1.5 %collective-permute-done.refs_1_ = f32[8,1024]{1,0:T(8,128)S(1)} collective-permute-done((f32[8,1024]{1,0:T(8,128)}, f32[8,1024]{1,0:T(8,128)S(1)}, u32[]{:S(2)}, u32[]{:S(2)}) %collective-permute-start) | collective-permute-done | bytes 32800 | tf_op jit(solution)/shard_map/ppermute | solution.py:185
  12.5 0.0 copy-start.2
  12.5 2.0 %collective-permute-done.1.refs_2_ = f32[8,1024]{1,0:T(8,128)S(1)} collective-permute-done((f32[8,1024]{1,0:T(8,128)}, f32[8,1024]{1,0:T(8,128)S(1)}, u32[]{:S(2)}, u32[]{:S(2)}) %collective-permute-start.1) | collective-permute-done | bytes 32800 | tf_op jit(solution)/shard_map/ppermute | solution.py:185
  14.5 0.0 copy-start.3
  14.5 0.5 %collective-permute-done.2.refs_3_ = f32[8,1024]{1,0:T(8,128)S(1)} collective-permute-done((f32[8,1024]{1,0:T(8,128)}, f32[8,1024]{1,0:T(8,128)S(1)}, u32[]{:S(2)}, u32[]{:S(2)}) %collective-permute-start.2) | collective-permute-done | bytes 32800 | tf_op jit(solution)/shard_map/ppermute | solution.py:185
  15.0 0.0 copy-start.4
  15.0 0.0 copy-done.2
  15.0 0.1 copy-done.3
  15.1 0.5 %copy-done.4 = f32[8,1024]{1,0:T(8,128)} copy-done((f32[8,1024]{1,0:T(8,128)}, f32[8,1024]{1,0:T(8,128)S(1)}, u32[]{:S(2)}) %copy-start.4) | copy-done | bytes 32792
  15.6 1.5 %mean_rows.1 = bf16[16,8,768]{2,1,0:T(8,128)(2,1)} custom-call(s32[1,3]{1,0:T(1,128)} %lens.3, f32[8,1024]{1,0:T(8,128)} %get-tuple-element.6.refs_0_, f32[8,1024]{1,0:T(8,128)} %copy-done.2, f32[8,1024]{1,0:T(8,128)} %copy-done.3, f32[8,1024]{1,0:T(8,128)} %copy-done.4), custom_call_target="tpu_custom_call" | custom-call | tf_op jit(solution)/shard_map/mean_rows/pallas_call | solution.py:187
  17.2 14.0 %all_to_all.5 = bf16[16,8,768]{2,1,0:T(8,128)(2,1)S(1)} all-to-all(bf16[16,8,768]{2,1,0:T(8,128)(2,1)} %mean_rows.1), channel_id=1, replica_groups=mesh['seq'=4,'pair'=4,'core'=2] {'seq','pair'}, dimensions={0} | all-to-all | bytes 393216 | tf_op jit(solution)/shard_map/all_to_all | solution.py:195
  31.2 0.0 copy-start
  31.2 0.0 collective-permute-start.3
  31.2 1.4 %collective-permute-done.3 = bf16[16,8,768]{2,1,0:T(8,128)(2,1)S(1)} collective-permute-done((bf16[16,8,768]{2,1,0:T(8,128)(2,1)S(1)}, bf16[16,8,768]{2,1,0:T(8,128)(2,1)S(1)}, u32[]{:S(2)}, u32[]{:S(2)}) %collective-permute-start.3) | collective-permute-done | bytes 196640 | tf_op jit(solution)/shard_map/ppermute | solution.py:196
  32.6 0.0 copy-start.1
  32.6 0.0 copy-done
  32.6 0.7 %copy-done.1 = bf16[16,8,768]{2,1,0:T(8,128)(2,1)} copy-done((bf16[16,8,768]{2,1,0:T(8,128)(2,1)}, bf16[16,8,768]{2,1,0:T(8,128)(2,1)S(1)}, u32[]{:S(2)}) %copy-start.1) | copy-done | bytes 196632
  33.3 3.6 %factor_tiles.1 = (f32[128,4096]{1,0:T(8,128)}, f32[128,4096]{1,0:T(8,128)}) custom-call(bf16[4,4,8,768]{3,2,1,0:T(8,128)(2,1)} %bitcast.2, bf16[4,4,8,768]{3,2,1,0:T(8,128)(2,1)} %bitcast.3), custom_call_target="tpu_custom_call" | custom-call | tf_op jit(solution)/shard_map/factor_tiles/pallas_call | solution.py:199
Async XLA Ops:
  6.4 6.1 %collective-permute-start = (f32[8,1024]{1,0:T(8,128)}, f32[8,1024]{1,0:T(8,128)S(1)}, u32[]{:S(2)}, u32[]{:S(2)}) collective-permute-start(f32[8,1024]{1,0:T(8,128)} %get-tuple-element.7), channel_id=1, source_target_pairs={{0,24},{8,16},{16,8},{24,0},{1,25},{9,17},{17,9},{25,1},{2,26},{10... | collective-permute-start | bytes 98312 | tf_op jit(solution)/shard_map/ppermute | solution.py:185
  10.4 4.1 %collective-permute-start.1 = (f32[8,1024]{1,0:T(8,128)}, f32[8,1024]{1,0:T(8,128)S(1)}, u32[]{:S(2)}, u32[]{:S(2)}) collective-permute-start(f32[8,1024]{1,0:T(8,128)} %get-tuple-element.8), channel_id=1, source_target_pairs={{0,16},{8,24},{16,0},{24,8},{1,17},{9,25},{17,1},{25,9},{2,18},{10... | collective-permute-start | bytes 98312 | tf_op jit(solution)/shard_map/ppermute | solution.py:185
  10.9 4.1 %collective-permute-start.2 = (f32[8,1024]{1,0:T(8,128)}, f32[8,1024]{1,0:T(8,128)S(1)}, u32[]{:S(2)}, u32[]{:S(2)}) collective-permute-start(f32[8,1024]{1,0:T(8,128)} %get-tuple-element.9), channel_id=1, source_target_pairs={{0,8},{8,0},{16,24},{24,16},{1,9},{9,1},{17,25},{25,17},{2,10},{10... | collective-permute-start | bytes 98312 | tf_op jit(solution)/shard_map/ppermute | solution.py:185
  12.5 2.5 %copy-start.2 = (f32[8,1024]{1,0:T(8,128)}, f32[8,1024]{1,0:T(8,128)S(1)}, u32[]{:S(2)}) copy-start(f32[8,1024]{1,0:T(8,128)S(1)} %collective-permute-done.refs_1_) | copy-start | bytes 98308
  14.5 0.6 %copy-start.3 = (f32[8,1024]{1,0:T(8,128)}, f32[8,1024]{1,0:T(8,128)S(1)}, u32[]{:S(2)}) copy-start(f32[8,1024]{1,0:T(8,128)S(1)} %collective-permute-done.1.refs_2_) | copy-start | bytes 98308
  15.0 0.6 %copy-start.4 = (f32[8,1024]{1,0:T(8,128)}, f32[8,1024]{1,0:T(8,128)S(1)}, u32[]{:S(2)}) copy-start(f32[8,1024]{1,0:T(8,128)S(1)} %collective-permute-done.2.refs_3_) | copy-start | bytes 98308
  31.2 1.4 %copy-start = (bf16[16,8,768]{2,1,0:T(8,128)(2,1)}, bf16[16,8,768]{2,1,0:T(8,128)(2,1)S(1)}, u32[]{:S(2)}) copy-start(bf16[16,8,768]{2,1,0:T(8,128)(2,1)S(1)} %all_to_all.5) | copy-start | bytes 589828
  31.2 1.4 %collective-permute-start.3 = (bf16[16,8,768]{2,1,0:T(8,128)(2,1)S(1)}, bf16[16,8,768]{2,1,0:T(8,128)(2,1)S(1)}, u32[]{:S(2)}, u32[]{:S(2)}) collective-permute-start(bf16[16,8,768]{2,1,0:T(8,128)(2,1)S(1)} %all_to_all.5), channel_id=1, source_target_pairs={{0,1},{1,0},{2,3},{3,2},{4,5},{5,4},{6,7},{7,6},{8,9},{9,8},{10,11... | collective-permute-start | bytes 589832 | tf_op jit(solution)/shard_map/ppermute | solution.py:196
  32.6 0.7 %copy-start.1 = (bf16[16,8,768]{2,1,0:T(8,128)(2,1)}, bf16[16,8,768]{2,1,0:T(8,128)(2,1)S(1)}, u32[]{:S(2)}) copy-start(bf16[16,8,768]{2,1,0:T(8,128)(2,1)S(1)} %collective-permute-done.3) | copy-start | bytes 589828

commit v2 on v1

v2 whole, which is shorter than its diff:
```python
import functools

import jax
import jax.numpy as jnp
from jax import lax
from jax.experimental import pallas as pl
from jax.experimental.pallas import tpu as pltpu
from jax.sharding import Mesh
from jax.sharding import PartitionSpec as P

LANES = 128
ROWS = 8
MIB = 1 << 20


def spare_split(rows, width):
    spare = ROWS - rows
    if spare <= 0 or rows % spare or (width * rows) % (ROWS * LANES):
        return width, 0
    kept = width * rows // ROWS
    tail = width - kept
    if tail % LANES:
        return width, 0
    return kept, tail


def partner(index, offset, count):
    if count & (count - 1) == 0:
        return index ^ offset
    return (index + offset) % count


def fold(values, rows, kept, tail):
    if not tail:
        return values
    row = lax.broadcasted_iota(jnp.int32, (ROWS, 1), 0)
    spare = ROWS - rows
    per = rows // spare
    pieces = []
    for k in range(per):
        piece = values[:, k * tail : (k + 1) * tail]
        for j in range(spare):
            piece = jnp.where(row == rows + j, values[j * per + k : j * per + k + 1, kept:], piece)
        pieces.append(piece)
    return jnp.concatenate(pieces, axis=1)


def unfold(block, rows, kept, tail):
    row = lax.broadcasted_iota(jnp.int32, (1, ROWS, 1), 1)
    spare = ROWS - rows
    per = rows // spare
    wide = block.astype(jnp.float32)
    rest = jnp.zeros((block.shape[0], ROWS, tail), jnp.float32)
    for j in range(spare):
        for k in range(per):
            source = wide[:, rows + j : rows + j + 1, k * tail : (k + 1) * tail]
            rest = jnp.where(row == j * per + k, source, rest)
    return rest.astype(block.dtype)


def segment_kernel(seq_count, chunk_count, offsets, slabs, kept, tail, act, grad, lens, *refs):
    outs = refs[: len(offsets)]
    act_buf, grad_buf, len_buf, act_sem, grad_sem, len_sem = refs[len(offsets) :]
    tokens = act.shape[1]
    slab = act_buf.shape[2]
    width = kept + tail
    rows = 2 * seq_count
    me = lax.axis_index("seq")
    len_copy = pltpu.make_async_copy(lens, len_buf, len_sem)
    len_copy.start()
    copies = []
    for slot, offset in enumerate(offsets):
        base = partner(me, offset, chunk_count) * width
        for part in range(slabs):
            at = slot * slabs + part
            cols = pl.ds(pl.multiple_of(base + part * slab, slab), slab)
            pair = (
                pltpu.make_async_copy(act.at[0, :, cols], act_buf.at[at], act_sem.at[at]),
                pltpu.make_async_copy(grad.at[0, :, cols], grad_buf.at[at], grad_sem.at[at]),
            )
            for copy in pair:
                copy.start()
            copies.append(pair)
    len_copy.wait()
    row = lax.broadcasted_iota(jnp.int32, (ROWS, tokens), 0)
    position = lax.broadcasted_iota(jnp.int32, (ROWS, tokens), 1) + me * tokens
    thin = lax.broadcasted_iota(jnp.int32, (ROWS, 1), 0)
    low = jnp.zeros((ROWS, tokens), jnp.int32)
    high = jnp.zeros((ROWS, tokens), jnp.int32)
    count = jnp.ones((ROWS, 1), jnp.float32)
    start = jnp.int32(0)
    for s in range(seq_count):
        size = len_buf[0, s]
        mine = (row == s) | (row == s + seq_count)
        low = jnp.where(mine, start, low)
        high = jnp.where(mine, start + size, high)
        count = jnp.where(thin == s, size.astype(jnp.float32), count)
        start = start + size
    member = (position >= low) & (position < high)
    act_member = jnp.where(member & (row < seq_count), 1.0, 0.0).astype(jnp.bfloat16)
    grad_member = jnp.where(member & (row >= seq_count), 1.0, 0.0).astype(jnp.bfloat16)
    for slot in range(len(offsets)):
        sums = []
        for part in range(slabs):
            at = slot * slabs + part
            for copy in copies[at]:
                copy.wait()
            both = jnp.dot(act_member, act_buf[at], preferred_element_type=jnp.float32)
            both += jnp.dot(grad_member, grad_buf[at], preferred_element_type=jnp.float32)
            sums.append(both)
        outs[slot][...] = fold(jnp.concatenate(sums, axis=1) / count, rows, kept, tail)


def spread_kernel(*refs):
    parts, out = refs[:-1], refs[-1]
    total = parts[0][...]
    for part in parts[1:]:
        total += part[...]
    total = total.astype(out.dtype)
    for g in range(out.shape[0]):
        out[g] = total


def factor_kernel(seq_count, total_seqs, kept, tail, near, far, act_out, grad_out, own, act_buf, grad_buf, act_sem, grad_sem):
    chunks, pairs = near.shape[0], near.shape[1]
    rows = 2 * seq_count
    width = kept + tail
    half = pairs * ROWS
    tile, piece = act_buf.shape[1:]

    def chunk(c):
        parts = []
        for ref in (near, far):
            block = ref[c]
            flat = block.reshape(half, kept)
            if tail:
                flat = jnp.concatenate([flat, unfold(block, rows, kept, tail).reshape(half, tail)], axis=1)
            parts.append(flat)
        return jnp.concatenate(parts, axis=0)

    seq = lax.axis_index("seq")
    own[...] = chunk(seq).astype(jnp.float32)
    first = (lax.axis_index("pair") * lax.axis_size("core") + lax.axis_index("core")) * tile
    span = max(tile, LANES)
    base = pl.multiple_of(first // LANES * LANES, LANES)
    left = own[:, pl.ds(base, span)]
    if tile < span:
        left = pltpu.roll(left, span - (first - base), 1)
    left = left.T[:tile]
    kind = lax.rem(lax.broadcasted_iota(jnp.int32, left.shape, 1), ROWS)
    act_left = jnp.where(kind < seq_count, left, 0.0)
    grad_left = jnp.where((kind >= seq_count) & (kind < rows), left, 0.0)
    left = jnp.concatenate([act_left, grad_left], axis=0).astype(jnp.bfloat16)
    copies = []
    for c in range(chunks):
        right = chunk(c)
        for part in range(width // piece):
            at = c * (width // piece) + part
            product = jnp.dot(left, right[:, part * piece : (part + 1) * piece], preferred_element_type=jnp.float32)
            product *= 1.0 / total_seqs
            act_buf[at] = product[:tile]
            grad_buf[at] = product[tile:]
            cols = pl.ds(at * piece, piece)
            pair = (
                pltpu.make_async_copy(act_buf.at[at], act_out.at[:, cols], act_sem.at[at]),
                pltpu.make_async_copy(grad_buf.at[at], grad_out.at[:, cols], grad_sem.at[at]),
            )
            for copy in pair:
                copy.start()
            copies.append(pair)
    for pair in copies:
        for copy in pair:
            copy.wait()


def local(activations, out_grads, lengths):
    chunks = lax.axis_size("seq")
    pairs = lax.axis_size("pair")
    cores = lax.axis_size("core")
    tokens, depth = activations.shape[1], activations.shape[2]
    seq_count = lengths.shape[1]
    width = depth // chunks
    slabs = 2 if width % (2 * LANES) == 0 else 1
    slab = width // slabs
    tile = depth // (chunks * pairs * cores)
    kept, tail = spare_split(2 * seq_count, width)
    vmem = pl.BlockSpec(memory_space=pltpu.VMEM)
    anywhere = pl.BlockSpec(memory_space=pl.ANY)
    held = [pltpu.with_memory_space_constraint(a, pltpu.HBM) for a in (activations, out_grads, lengths)]

    def segment_sums(offsets):
        count = len(offsets) * slabs
        return pl.pallas_call(
            functools.partial(segment_kernel, seq_count, chunks, offsets, slabs, kept, tail),
            out_shape=[jax.ShapeDtypeStruct((ROWS, kept), jnp.float32)] * len(offsets),
            in_specs=[anywhere] * 3,
            out_specs=[vmem] * len(offsets),
            scratch_shapes=[
                pltpu.VMEM((count, tokens, slab), jnp.bfloat16),
                pltpu.VMEM((count, tokens, slab), jnp.bfloat16),
                pltpu.SMEM(lengths.shape, jnp.int32),
                pltpu.SemaphoreType.DMA((count,)),
                pltpu.SemaphoreType.DMA((count,)),
                pltpu.SemaphoreType.DMA,
            ],
            compiler_params=pltpu.CompilerParams(vmem_limit_bytes=20 * MIB),
            cost_estimate=pl.CostEstimate(
                flops=4 * ROWS * tokens * width * len(offsets),
                bytes_accessed=4 * tokens * width * len(offsets),
                transcendentals=0,
            ),
            name="segment_sums",
        )(*held)

    offsets = list(range(chunks - 1, 0, -1))
    sent = segment_sums(offsets)
    arrived = []
    for offset, part in zip(offsets, sent):
        ring = [(i, partner(i, offset, chunks)) for i in range(chunks)]
        arrived.append(lax.ppermute(part, "seq", ring))
    arrived += segment_sums([0])

    spread = pl.pallas_call(
        spread_kernel,
        out_shape=jax.ShapeDtypeStruct((chunks * pairs, ROWS, kept), jnp.bfloat16),
        in_specs=[vmem] * chunks,
        out_specs=vmem,
        compiler_params=pltpu.CompilerParams(vmem_limit_bytes=8 * MIB),
        name="mean_rows",
    )(*arrived)

    near = lax.all_to_all(spread, ("seq", "pair"), 0, 0, tiled=True)
    far = lax.ppermute(near, "core", [(i, (i + 1) % cores) for i in range(cores)])
    near, far = (a.reshape(chunks, pairs, ROWS, kept) for a in (near, far))

    piece = slab
    return pl.pallas_call(
        functools.partial(factor_kernel, seq_count, seq_count * pairs * cores, kept, tail),
        out_shape=[jax.ShapeDtypeStruct((tile, depth), jnp.float32)] * 2,
        in_specs=[vmem] * 2,
        out_specs=[anywhere] * 2,
        scratch_shapes=[
            pltpu.VMEM((2 * pairs * ROWS, width), jnp.float32),
            pltpu.VMEM((depth // piece, tile, piece), jnp.float32),
            pltpu.VMEM((depth // piece, tile, piece), jnp.float32),
            pltpu.SemaphoreType.DMA((depth // piece,)),
            pltpu.SemaphoreType.DMA((depth // piece,)),
        ],
        compiler_params=pltpu.CompilerParams(vmem_limit_bytes=20 * MIB),
        name="factor_tiles",
    )(near, far)


def solution(mesh):
    batch = mesh.shape["batch"]
    split = Mesh(mesh.devices.reshape(mesh.shape["seq"], batch // 2, 2), ("seq", "pair", "core"))
    groups = ("pair", "core")
    in_specs = (P(groups, "seq", None), P(groups, "seq", None), P(groups, None))
    out_specs = (P(("seq",) + groups, None), P(("seq",) + groups, None))

    def program(activations, out_grads, lengths):
        return tuple(jax.shard_map(local, mesh=split, in_specs=in_specs, out_specs=out_specs, check_vma=False)(activations, out_grads, lengths))

    return program
```

time: 37.2 us -> 31.3 us (0.84)
  waiting for transfers between devices: 5.42 us -> 2.89 us
  Pallas kernels: 10.9 us -> 8.88 us
  local copies, waits for them, and re-layouts: 1.27 us -> 0 us
    ppermute x3, waiting for transfers between devices: 3.98 us -> 1.45 us  [local(): arrived.append(lax.ppermute(part, 'seq', ring))]
    unnamed x10 -> x0, local copies, waits for them, and re-layouts: 1.27 us -> none
    pallas_call x1, Pallas kernels: 3.64 us -> 2.43 us  [local(): pl.pallas_call(functools.partial(factor_kernel, seq_count, seq_count * pa...]
    pallas_call x2 -> x3, Pallas kernels: 7.3 us -> 6.45 us  [the longest x2 6.43 us: segment_sums(): pl.pallas_call(functools.partial(segment_kernel, seq_count, chunks, offse...]
  transfers between devices with their start and end apart: 4 -> 4, of which waited for: 4 -> 3; matrix products, arithmetic and copies ran while one was open for 0% -> 0% of each run, Pallas kernels for 0% -> 7%
where the time goes in v2:
time: 31.3 us; the launch traced here: 31.1 us
  blocking collectives  14.1 us (45%)
  Pallas kernels  8.88 us (28%)
  starting transfers between devices  4.63 us (15%)
  waiting for transfers between devices  2.89 us (9%)
  between operations  0.66 us (2%)
    all_to_all x1, blocking collectives, local(): near = lax.all_to_all(spread, ('seq', 'pair'), 0, 0, tiled=True)  14.1 us
    pallas_call x2, Pallas kernels, segment_sums(): pl.pallas_call(functools.partial(segment_kernel, seq_count, chunks, offse...  6.43 us
    ppermute x3, starting transfers between devices, local(): arrived.append(lax.ppermute(part, 'seq', ring))  4.63 us
    pallas_call x1, Pallas kernels, local(): pl.pallas_call(functools.partial(factor_kernel, seq_count, seq_count * pa...  2.43 us
    ppermute x3, waiting for transfers between devices, local(): arrived.append(lax.ppermute(part, 'seq', ring))  1.45 us
    ppermute x1, waiting for transfers between devices, local(): lax.ppermute(near, 'core', [(i, (i + 1) % cores) for i in range(cores)])  1.44 us
  transfers between devices with their start and end apart: 4, of which 3 were waited for; matrix products, arithmetic and copies ran while one was open for 0% of the time, Pallas kernels for 7%

profile of v2, /device:TPU:0, one launch (start us, length us, event | category | flops | bytes accessed | tf_op | source)
XLA Modules:
  0.0 31.1 jit_solution(11111142795505811106)
XLA Ops:
  0.6 4.2 %segment_sums.2 = (f32[8,768]{1,0:T(8,128)S(1)}, f32[8,768]{1,0:T(8,128)S(1)}, f32[8,768]{1,0:T(8,128)S(1)}) custom-call(bf16[1,768,4096]{2,1,0:T(8,128)(2,1)} %act.3, bf16[1,768,4096]{2,1,0:T(8,128)(2,1)} %grad.3, s32[1,3]{1,0:T(1,128)} %lens.3), custom_call_target="tpu_custom_call" | custom-call | flops 75497472 | bytes 9437184 | tf_op jit(solution)/shard_map/segment_sums/pallas_call | solution.py:193
  4.8 4.0 %collective-permute-start = (f32[8,768]{1,0:T(8,128)S(1)}, f32[8,768]{1,0:T(8,128)S(1)}, u32[]{:S(2)}, u32[]{:S(2)}) collective-permute-start(f32[8,768]{1,0:T(8,128)S(1)} %get-tuple-element.5), channel_id=1, source_target_pairs={{0,24},{8,16},{16,8},{24,0},{1,25},{9,17},{17,9},{25,1},{2,26},{10... | collective-permute-start | bytes 73736 | tf_op jit(solution)/shard_map/ppermute | solution.py:220
  8.8 0.5 %collective-permute-start.1 = (f32[8,768]{1,0:T(8,128)S(1)}, f32[8,768]{1,0:T(8,128)S(1)}, u32[]{:S(2)}, u32[]{:S(2)}) collective-permute-start(f32[8,768]{1,0:T(8,128)S(1)} %get-tuple-element.6), channel_id=1, source_target_pairs={{0,16},{8,24},{16,0},{24,8},{1,17},{9,25},{17,1},{25,9},{2,18},{10... | collective-permute-start | bytes 73736 | tf_op jit(solution)/shard_map/ppermute | solution.py:220
  9.3 0.1 collective-permute-start.2
  9.5 2.2 %segment_sums.3.refs_3_ = f32[8,768]{1,0:T(8,128)S(1)} custom-call(bf16[1,768,4096]{2,1,0:T(8,128)(2,1)} %act.3, bf16[1,768,4096]{2,1,0:T(8,128)(2,1)} %grad.3, s32[1,3]{1,0:T(1,128)} %lens.3), custom_call_target="tpu_custom_call" | custom-call | flops 25165824 | bytes 3145728 | tf_op jit(solution)/shard_map/segment_sums/pallas_call | solution.py:193
  11.7 0.0 collective-permute-done.refs_0_
  11.7 0.9 %collective-permute-done.1.refs_1_ = f32[8,768]{1,0:T(8,128)S(1)} collective-permute-done((f32[8,768]{1,0:T(8,128)S(1)}, f32[8,768]{1,0:T(8,128)S(1)}, u32[]{:S(2)}, u32[]{:S(2)}) %collective-permute-start.1) | collective-permute-done | bytes 24608 | tf_op jit(solution)/shard_map/ppermute | solution.py:220
  12.7 0.5 %collective-permute-done.2.refs_2_ = f32[8,768]{1,0:T(8,128)S(1)} collective-permute-done((f32[8,768]{1,0:T(8,128)S(1)}, f32[8,768]{1,0:T(8,128)S(1)}, u32[]{:S(2)}, u32[]{:S(2)}) %collective-permute-start.2) | collective-permute-done | bytes 24608 | tf_op jit(solution)/shard_map/ppermute | solution.py:220
  13.2 14.1 %all_to_all.5 = bf16[16,8,768]{2,1,0:T(8,128)(2,1)S(1)} all-to-all(bf16[16,8,768]{2,1,0:T(8,128)(2,1)S(1)} %mean_rows.1), channel_id=1, replica_groups=mesh['seq'=4,'pair'=4,'core'=2] {'seq','pair'}, dimensions={0} | all-to-all | bytes 393216 | tf_op jit(solution)/shard_map/all_to_all | solution.py:232
  27.3 0.0 collective-permute-start.3
  27.3 1.4 %collective-permute-done.3 = bf16[16,8,768]{2,1,0:T(8,128)(2,1)S(1)} collective-permute-done((bf16[16,8,768]{2,1,0:T(8,128)(2,1)S(1)}, bf16[16,8,768]{2,1,0:T(8,128)(2,1)S(1)}, u32[]{:S(2)}, u32[]{:S(2)}) %collective-permute-start.3) | collective-permute-done | bytes 196640 | tf_op jit(solution)/shard_map/ppermute | solution.py:233
  28.7 2.4 %factor_tiles.1 = (f32[128,4096]{1,0:T(8,128)}, f32[128,4096]{1,0:T(8,128)}) custom-call(bf16[4,4,8,768]{3,2,1,0:T(8,128)(2,1)S(1)} %bitcast.2, bf16[4,4,8,768]{3,2,1,0:T(8,128)(2,1)S(1)} %bitcast.3), custom_call_target="tpu_custom_call" | custom-call | tf_op jit(solution)/shard_map/factor_tiles/pallas_call | solution.py:237
  (1 shorter events, 0.0 us)
Async XLA Ops:
  4.8 6.9 %collective-permute-start = (f32[8,768]{1,0:T(8,128)S(1)}, f32[8,768]{1,0:T(8,128)S(1)}, u32[]{:S(2)}, u32[]{:S(2)}) collective-permute-start(f32[8,768]{1,0:T(8,128)S(1)} %get-tuple-element.5), channel_id=1, source_target_pairs={{0,24},{8,16},{16,8},{24,0},{1,25},{9,17},{17,9},{25,1},{2,26},{10... | collective-permute-start | bytes 73736 | tf_op jit(solution)/shard_map/ppermute | solution.py:220
  8.8 3.8 %collective-permute-start.1 = (f32[8,768]{1,0:T(8,128)S(1)}, f32[8,768]{1,0:T(8,128)S(1)}, u32[]{:S(2)}, u32[]{:S(2)}) collective-permute-start(f32[8,768]{1,0:T(8,128)S(1)} %get-tuple-element.6), channel_id=1, source_target_pairs={{0,16},{8,24},{16,0},{24,8},{1,17},{9,25},{17,1},{25,9},{2,18},{10... | collective-permute-start | bytes 73736 | tf_op jit(solution)/shard_map/ppermute | solution.py:220
  9.3 3.8 %collective-permute-start.2 = (f32[8,768]{1,0:T(8,128)S(1)}, f32[8,768]{1,0:T(8,128)S(1)}, u32[]{:S(2)}, u32[]{:S(2)}) collective-permute-start(f32[8,768]{1,0:T(8,128)S(1)} %get-tuple-element.7), channel_id=1, source_target_pairs={{0,8},{8,0},{16,24},{24,16},{1,9},{9,1},{17,25},{25,17},{2,10},{10... | collective-permute-start | bytes 73736 | tf_op jit(solution)/shard_map/ppermute | solution.py:220
  27.3 1.4 %collective-permute-start.3 = (bf16[16,8,768]{2,1,0:T(8,128)(2,1)S(1)}, bf16[16,8,768]{2,1,0:T(8,128)(2,1)S(1)}, u32[]{:S(2)}, u32[]{:S(2)}) collective-permute-start(bf16[16,8,768]{2,1,0:T(8,128)(2,1)S(1)} %all_to_all.5), channel_id=1, source_target_pairs={{0,1},{1,0},{2,3},{3,2},{4,5},{5,4},{6,7},{7,6},{8,9},{9,8},{10,11... | collective-permute-start | bytes 589832 | tf_op jit(solution)/shard_map/ppermute | solution.py:233

commit v3 on v2

--- a/solution.py
+++ b/solution.py
@@ -62,7 +62,7 @@
     outs = refs[: len(offsets)]
     act_buf, grad_buf, len_buf, act_sem, grad_sem, len_sem = refs[len(offsets) :]
     tokens = act.shape[1]
-    slab = act_buf.shape[2]
+    slab = act_buf.shape[1]
     width = kept + tail
     rows = 2 * seq_count
     me = lax.axis_index("seq")
@@ -71,12 +71,13 @@
     copies = []
     for slot, offset in enumerate(offsets):
         base = partner(me, offset, chunk_count) * width
+        cols = pl.ds(pl.multiple_of(base, width), width)
         for part in range(slabs):
             at = slot * slabs + part
-            cols = pl.ds(pl.multiple_of(base + part * slab, slab), slab)
+            span = pl.ds(part * slab, slab)
             pair = (
-                pltpu.make_async_copy(act.at[0, :, cols], act_buf.at[at], act_sem.at[at]),
-                pltpu.make_async_copy(grad.at[0, :, cols], grad_buf.at[at], grad_sem.at[at]),
+                pltpu.make_async_copy(act.at[0, span, cols], act_buf.at[at], act_sem.at[at]),
+                pltpu.make_async_copy(grad.at[0, span, cols], grad_buf.at[at], grad_sem.at[at]),
             )
             for copy in pair:
                 copy.start()
@@ -100,15 +101,14 @@
     act_member = jnp.where(member & (row < seq_count), 1.0, 0.0).astype(jnp.bfloat16)
     grad_member = jnp.where(member & (row >= seq_count), 1.0, 0.0).astype(jnp.bfloat16)
     for slot in range(len(offsets)):
-        sums = []
+        sums = jnp.zeros((ROWS, width), jnp.float32)
         for part in range(slabs):
             at = slot * slabs + part
-            for copy in copies[at]:
+            span = slice(part * slab, (part + 1) * slab)
+            for member, buf, copy in zip((act_member, grad_member), (act_buf, grad_buf), copies[at]):
                 copy.wait()
-            both = jnp.dot(act_member, act_buf[at], preferred_element_type=jnp.float32)
-            both += jnp.dot(grad_member, grad_buf[at], preferred_element_type=jnp.float32)
-            sums.append(both)
-        outs[slot][...] = fold(jnp.concatenate(sums, axis=1) / count, rows, kept, tail)
+                sums += jnp.dot(member[:, span], buf[at], preferred_element_type=jnp.float32)
+        outs[slot][...] = fold(sums / count, rows, kept, tail)
 
 
 def spread_kernel(*refs):
@@ -131,7 +131,7 @@
     def chunk(c):
         parts = []
         for ref in (near, far):
-            block = ref[c]
+            block = ref[chunks - 1 - c]
             flat = block.reshape(half, kept)
             if tail:
                 flat = jnp.concatenate([flat, unfold(block, rows, kept, tail).reshape(half, tail)], axis=1)
@@ -180,8 +180,8 @@
     tokens, depth = activations.shape[1], activations.shape[2]
     seq_count = lengths.shape[1]
     width = depth // chunks
-    slabs = 2 if width % (2 * LANES) == 0 else 1
-    slab = width // slabs
+    slabs = next(n for n in (2, 1) if tokens % (n * LANES) == 0 or n == 1)
+    slab = tokens // slabs
     tile = depth // (chunks * pairs * cores)
     kept, tail = spare_split(2 * seq_count, width)
     vmem = pl.BlockSpec(memory_space=pltpu.VMEM)
@@ -196,8 +196,8 @@
             in_specs=[anywhere] * 3,
             out_specs=[vmem] * len(offsets),
             scratch_shapes=[
-                pltpu.VMEM((count, tokens, slab), jnp.bfloat16),
-                pltpu.VMEM((count, tokens, slab), jnp.bfloat16),
+                pltpu.VMEM((count, slab, width), jnp.bfloat16),
+                pltpu.VMEM((count, slab, width), jnp.bfloat16),
                 pltpu.SMEM(lengths.shape, jnp.int32),
                 pltpu.SemaphoreType.DMA((count,)),
                 pltpu.SemaphoreType.DMA((count,)),
@@ -229,11 +229,13 @@
         name="mean_rows",
     )(*arrived)
 
-    near = lax.all_to_all(spread, ("seq", "pair"), 0, 0, tiled=True)
+    order = list(range(pairs - 1, -1, -2)) + list(range(pairs - 2, -1, -2))
+    members = [[(s * pairs + p) * cores + c for s in range(chunks - 1, -1, -1) for p in order] for c in range(cores)]
+    near = lax.all_to_all(spread, ("seq", "pair", "core"), 0, 0, axis_index_groups=members, tiled=True)
     far = lax.ppermute(near, "core", [(i, (i + 1) % cores) for i in range(cores)])
     near, far = (a.reshape(chunks, pairs, ROWS, kept) for a in (near, far))
 
-    piece = slab
+    piece = width // 2 if width % (2 * LANES) == 0 else width
     return pl.pallas_call(
         functools.partial(factor_kernel, seq_count, seq_count * pairs * cores, kept, tail),
         out_shape=[jax.ShapeDtypeStruct((tile, depth), jnp.float32)] * 2,

time: 31.3 us -> 28.4 us (0.907)
  blocking collectives: 14.1 us -> 11.3 us
    all_to_all x1, blocking collectives: 14.1 us -> 11.3 us  [local(): lax.all_to_all(spread, ('seq', 'pair', 'core'), 0, 0, axis_index_groups=m...]
  transfers between devices with their start and end apart: 4 -> 4, of which waited for: 3 -> 3; matrix products, arithmetic and copies ran while one was open for 0% -> 0% of each run, Pallas kernels for 7% -> 8%
where the time goes in v3:
time: 28.4 us; the launch traced here: 28.2 us
  blocking collectives  11.3 us (40%)
  Pallas kernels  8.64 us (30%)
  starting transfers between devices  4.63 us (16%)
  waiting for transfers between devices  3 us (11%)
  between operations  0.66 us (2%)
    all_to_all x1, blocking collectives, local(): lax.all_to_all(spread, ('seq', 'pair', 'core'), 0, 0, axis_index_groups=m...  11.3 us
    pallas_call x2, Pallas kernels, segment_sums(): pl.pallas_call(functools.partial(segment_kernel, seq_count, chunks, offse...  6.19 us
    ppermute x3, starting transfers between devices, local(): arrived.append(lax.ppermute(part, 'seq', ring))  4.63 us
    pallas_call x1, Pallas kernels, local(): pl.pallas_call(functools.partial(factor_kernel, seq_count, seq_count * pa...  2.43 us
    ppermute x3, waiting for transfers between devices, local(): arrived.append(lax.ppermute(part, 'seq', ring))  1.56 us
    ppermute x1, waiting for transfers between devices, local(): lax.ppermute(near, 'core', [(i, (i + 1) % cores) for i in range(cores)])  1.44 us
  transfers between devices with their start and end apart: 4, of which 3 were waited for; matrix products, arithmetic and copies ran while one was open for 0% of the time, Pallas kernels for 8%

profile of v3, /device:TPU:0, one launch (start us, length us, event | category | flops | bytes accessed | tf_op | source)
XLA Modules:
  0.0 28.2 jit_solution(3186017278750953825)
XLA Ops:
  0.6 4.1 %segment_sums.2 = (f32[8,768]{1,0:T(8,128)S(1)}, f32[8,768]{1,0:T(8,128)S(1)}, f32[8,768]{1,0:T(8,128)S(1)}) custom-call(bf16[1,768,4096]{2,1,0:T(8,128)(2,1)} %act.3, bf16[1,768,4096]{2,1,0:T(8,128)(2,1)} %grad.3, s32[1,3]{1,0:T(1,128)} %lens.3), custom_call_target="tpu_custom_call" | custom-call | flops 75497472 | bytes 9437184 | tf_op jit(solution)/shard_map/segment_sums/pallas_call | solution.py:193
  4.7 4.0 %collective-permute-start = (f32[8,768]{1,0:T(8,128)S(1)}, f32[8,768]{1,0:T(8,128)S(1)}, u32[]{:S(2)}, u32[]{:S(2)}) collective-permute-start(f32[8,768]{1,0:T(8,128)S(1)} %get-tuple-element.5), channel_id=1, source_target_pairs={{0,24},{8,16},{16,8},{24,0},{1,25},{9,17},{17,9},{25,1},{2,26},{10... | collective-permute-start | bytes 73736 | tf_op jit(solution)/shard_map/ppermute | solution.py:220
  8.7 0.5 %collective-permute-start.1 = (f32[8,768]{1,0:T(8,128)S(1)}, f32[8,768]{1,0:T(8,128)S(1)}, u32[]{:S(2)}, u32[]{:S(2)}) collective-permute-start(f32[8,768]{1,0:T(8,128)S(1)} %get-tuple-element.6), channel_id=1, source_target_pairs={{0,16},{8,24},{16,0},{24,8},{1,17},{9,25},{17,1},{25,9},{2,18},{10... | collective-permute-start | bytes 73736 | tf_op jit(solution)/shard_map/ppermute | solution.py:220
  9.2 0.1 collective-permute-start.2
  9.3 2.1 %segment_sums.3.refs_3_ = f32[8,768]{1,0:T(8,128)S(1)} custom-call(bf16[1,768,4096]{2,1,0:T(8,128)(2,1)} %act.3, bf16[1,768,4096]{2,1,0:T(8,128)(2,1)} %grad.3, s32[1,3]{1,0:T(1,128)} %lens.3), custom_call_target="tpu_custom_call" | custom-call | flops 25165824 | bytes 3145728 | tf_op jit(solution)/shard_map/segment_sums/pallas_call | solution.py:193
  11.5 0.0 collective-permute-done.refs_0_
  11.5 1.0 %collective-permute-done.1.refs_1_ = f32[8,768]{1,0:T(8,128)S(1)} collective-permute-done((f32[8,768]{1,0:T(8,128)S(1)}, f32[8,768]{1,0:T(8,128)S(1)}, u32[]{:S(2)}, u32[]{:S(2)}) %collective-permute-start.1) | collective-permute-done | bytes 24608 | tf_op jit(solution)/shard_map/ppermute | solution.py:220
  12.5 0.5 %collective-permute-done.2.refs_2_ = f32[8,768]{1,0:T(8,128)S(1)} collective-permute-done((f32[8,768]{1,0:T(8,128)S(1)}, f32[8,768]{1,0:T(8,128)S(1)}, u32[]{:S(2)}, u32[]{:S(2)}) %collective-permute-start.2) | collective-permute-done | bytes 24608 | tf_op jit(solution)/shard_map/ppermute | solution.py:220
  13.1 11.3 %all_to_all.5 = bf16[16,8,768]{2,1,0:T(8,128)(2,1)S(1)} all-to-all(bf16[16,8,768]{2,1,0:T(8,128)(2,1)S(1)} %mean_rows.1), channel_id=1, replica_groups={{30,26,28,24,22,18,20,16,14,10,12,8,6,2,4,0},{31,27,29,25,23,19,21,17,1..., dimensions={0} | all-to-all | bytes 393216 | tf_op jit(solution)/shard_map/all_to_all | solution.py:234
  24.3 0.0 collective-permute-start.3
  24.3 1.4 %collective-permute-done.3 = bf16[16,8,768]{2,1,0:T(8,128)(2,1)S(1)} collective-permute-done((bf16[16,8,768]{2,1,0:T(8,128)(2,1)S(1)}, bf16[16,8,768]{2,1,0:T(8,128)(2,1)S(1)}, u32[]{:S(2)}, u32[]{:S(2)}) %collective-permute-start.3) | collective-permute-done | bytes 196640 | tf_op jit(solution)/shard_map/ppermute | solution.py:235
  25.8 2.4 %factor_tiles.1 = (f32[128,4096]{1,0:T(8,128)}, f32[128,4096]{1,0:T(8,128)}) custom-call(bf16[4,4,8,768]{3,2,1,0:T(8,128)(2,1)S(1)} %bitcast.2, bf16[4,4,8,768]{3,2,1,0:T(8,128)(2,1)S(1)} %bitcast.3), custom_call_target="tpu_custom_call" | custom-call | tf_op jit(solution)/shard_map/factor_tiles/pallas_call | solution.py:239
  (1 shorter events, 0.0 us)
Async XLA Ops:
  4.7 6.8 %collective-permute-start = (f32[8,768]{1,0:T(8,128)S(1)}, f32[8,768]{1,0:T(8,128)S(1)}, u32[]{:S(2)}, u32[]{:S(2)}) collective-permute-start(f32[8,768]{1,0:T(8,128)S(1)} %get-tuple-element.5), channel_id=1, source_target_pairs={{0,24},{8,16},{16,8},{24,0},{1,25},{9,17},{17,9},{25,1},{2,26},{10... | collective-permute-start | bytes 73736 | tf_op jit(solution)/shard_map/ppermute | solution.py:220
  8.7 3.8 %collective-permute-start.1 = (f32[8,768]{1,0:T(8,128)S(1)}, f32[8,768]{1,0:T(8,128)S(1)}, u32[]{:S(2)}, u32[]{:S(2)}) collective-permute-start(f32[8,768]{1,0:T(8,128)S(1)} %get-tuple-element.6), channel_id=1, source_target_pairs={{0,16},{8,24},{16,0},{24,8},{1,17},{9,25},{17,1},{25,9},{2,18},{10... | collective-permute-start | bytes 73736 | tf_op jit(solution)/shard_map/ppermute | solution.py:220
  9.2 3.8 %collective-permute-start.2 = (f32[8,768]{1,0:T(8,128)S(1)}, f32[8,768]{1,0:T(8,128)S(1)}, u32[]{:S(2)}, u32[]{:S(2)}) collective-permute-start(f32[8,768]{1,0:T(8,128)S(1)} %get-tuple-element.7), channel_id=1, source_target_pairs={{0,8},{8,0},{16,24},{24,16},{1,9},{9,1},{17,25},{25,17},{2,10},{10... | collective-permute-start | bytes 73736 | tf_op jit(solution)/shard_map/ppermute | solution.py:220
  24.3 1.4 %collective-permute-start.3 = (bf16[16,8,768]{2,1,0:T(8,128)(2,1)S(1)}, bf16[16,8,768]{2,1,0:T(8,128)(2,1)S(1)}, u32[]{:S(2)}, u32[]{:S(2)}) collective-permute-start(bf16[16,8,768]{2,1,0:T(8,128)(2,1)S(1)} %all_to_all.5), channel_id=1, source_target_pairs={{0,1},{1,0},{2,3},{3,2},{4,5},{5,4},{6,7},{7,6},{8,9},{9,8},{10,11... | collective-permute-start | bytes 589832 | tf_op jit(solution)/shard_map/ppermute | solution.py:235

commit v4 on v3

--- a/solution.py
+++ b/solution.py
@@ -10,6 +10,7 @@
 
 LANES = 128
 ROWS = 8
+EVEN, TAPER = (1, 1), (3, 2, 1)
 MIB = 1 << 20
 
 
@@ -22,6 +23,12 @@
     if tail % LANES:
         return width, 0
     return kept, tail
+
+
+def spans(total, last):
+    shares = TAPER if last else EVEN
+    edges = [sum(shares[:i]) * total // sum(shares) // LANES * LANES for i in range(len(shares))] + [total]
+    return [(a, b) for a, b in zip(edges, edges[1:]) if b > a]
 
 
 def partner(index, offset, count):
@@ -62,26 +69,25 @@
     outs = refs[: len(offsets)]
     act_buf, grad_buf, len_buf, act_sem, grad_sem, len_sem = refs[len(offsets) :]
     tokens = act.shape[1]
-    slab = act_buf.shape[1]
     width = kept + tail
     rows = 2 * seq_count
     me = lax.axis_index("seq")
     len_copy = pltpu.make_async_copy(lens, len_buf, len_sem)
     len_copy.start()
-    copies = []
+    copies = {}
     for slot, offset in enumerate(offsets):
         base = partner(me, offset, chunk_count) * width
         cols = pl.ds(pl.multiple_of(base, width), width)
-        for part in range(slabs):
+        for part, (first, last) in enumerate(spans(tokens, slot == len(offsets) - 1)):
             at = slot * slabs + part
-            span = pl.ds(part * slab, slab)
+            span = pl.ds(first, last - first)
             pair = (
-                pltpu.make_async_copy(act.at[0, span, cols], act_buf.at[at], act_sem.at[at]),
-                pltpu.make_async_copy(grad.at[0, span, cols], grad_buf.at[at], grad_sem.at[at]),
+                pltpu.make_async_copy(act.at[0, span, cols], act_buf.at[slot, span], act_sem.at[at]),
+                pltpu.make_async_copy(grad.at[0, span, cols], grad_buf.at[slot, span], grad_sem.at[at]),
             )
             for copy in pair:
                 copy.start()
-            copies.append(pair)
+            copies[slot, part] = pair
     len_copy.wait()
     row = lax.broadcasted_iota(jnp.int32, (ROWS, tokens), 0)
     position = lax.broadcasted_iota(jnp.int32, (ROWS, tokens), 1) + me * tokens
@@ -102,12 +108,10 @@
     grad_member = jnp.where(member & (row >= seq_count), 1.0, 0.0).astype(jnp.bfloat16)
     for slot in range(len(offsets)):
         sums = jnp.zeros((ROWS, width), jnp.float32)
-        for part in range(slabs):
-            at = slot * slabs + part
-            span = slice(part * slab, (part + 1) * slab)
-            for member, buf, copy in zip((act_member, grad_member), (act_buf, grad_buf), copies[at]):
+        for part, (first, last) in enumerate(spans(tokens, slot == len(offsets) - 1)):
+            for member, buf, copy in zip((act_member, grad_member), (act_buf, grad_buf), copies[slot, part]):
                 copy.wait()
-                sums += jnp.dot(member[:, span], buf[at], preferred_element_type=jnp.float32)
+                sums += jnp.dot(member[:, first:last], buf[slot, first:last], preferred_element_type=jnp.float32)
         outs[slot][...] = fold(sums / count, rows, kept, tail)
 
 
@@ -121,25 +125,20 @@
         out[g] = total
 
 
-def factor_kernel(seq_count, total_seqs, kept, tail, near, far, act_out, grad_out, own, act_buf, grad_buf, act_sem, grad_sem):
-    chunks, pairs = near.shape[0], near.shape[1]
+def tile_products(seq_count, kept, tail, tile, piece, gathered, own, put):
+    chunks, pairs = gathered.shape[0], gathered.shape[1]
     rows = 2 * seq_count
     width = kept + tail
-    half = pairs * ROWS
-    tile, piece = act_buf.shape[1:]
+    depth = pairs * ROWS
 
     def chunk(c):
-        parts = []
-        for ref in (near, far):
-            block = ref[chunks - 1 - c]
-            flat = block.reshape(half, kept)
-            if tail:
-                flat = jnp.concatenate([flat, unfold(block, rows, kept, tail).reshape(half, tail)], axis=1)
-            parts.append(flat)
-        return jnp.concatenate(parts, axis=0)
-
-    seq = lax.axis_index("seq")
-    own[...] = chunk(seq).astype(jnp.float32)
+        block = gathered[chunks - 1 - c]
+        flat = block.reshape(depth, kept)
+        if tail:
+            flat = jnp.concatenate([flat, unfold(block, rows, kept, tail).reshape(depth, tail)], axis=1)
+        return flat
+
+    own[...] = chunk(lax.axis_index("seq")).astype(jnp.float32)
     first = (lax.axis_index("pair") * lax.axis_size("core") + lax.axis_index("core")) * tile
     span = max(tile, LANES)
     base = pl.multiple_of(first // LANES * LANES, LANES)
@@ -151,26 +150,37 @@
     act_left = jnp.where(kind < seq_count, left, 0.0)
     grad_left = jnp.where((kind >= seq_count) & (kind < rows), left, 0.0)
     left = jnp.concatenate([act_left, grad_left], axis=0).astype(jnp.bfloat16)
-    copies = []
     for c in range(chunks):
         right = chunk(c)
         for part in range(width // piece):
-            at = c * (width // piece) + part
-            product = jnp.dot(left, right[:, part * piece : (part + 1) * piece], preferred_element_type=jnp.float32)
-            product *= 1.0 / total_seqs
-            act_buf[at] = product[:tile]
-            grad_buf[at] = product[tile:]
-            cols = pl.ds(at * piece, piece)
-            pair = (
-                pltpu.make_async_copy(act_buf.at[at], act_out.at[:, cols], act_sem.at[at]),
-                pltpu.make_async_copy(grad_buf.at[at], grad_out.at[:, cols], grad_sem.at[at]),
-            )
-            for copy in pair:
-                copy.start()
-            copies.append(pair)
-    for pair in copies:
-        for copy in pair:
-            copy.wait()
+            cols = right[:, part * piece : (part + 1) * piece]
+            put(c * (width // piece) + part, jnp.dot(left, cols, preferred_element_type=jnp.float32))
+
+
+def near_kernel(seq_count, kept, tail, tile, near, share, own):
+    def put(at, product):
+        share[at] = product
+
+    tile_products(seq_count, kept, tail, tile, share.shape[2], near, own, put)
+
+
+def far_kernel(seq_count, total_seqs, kept, tail, far, share, act_out, grad_out, own, act_buf, grad_buf, act_sem, grad_sem):
+    tile, piece = act_buf.shape[1:]
+    copies = []
+
+    def put(at, product):
+        product = (product + share[at]) * (1.0 / total_seqs)
+        act_buf[at] = product[:tile]
+        grad_buf[at] = product[tile:]
+        cols = pl.ds(at * piece, piece)
+        for buf, out, sem in ((act_buf, act_out, act_sem), (grad_buf, grad_out, grad_sem)):
+            copy = pltpu.make_async_copy(buf.at[at], out.at[:, cols], sem.at[at])
+            copy.start()
+            copies.append(copy)
+
+    tile_products(seq_count, kept, tail, tile, piece, far, own, put)
+    for copy in copies:
+        copy.wait()
 
 
 def local(activations, out_grads, lengths):
@@ -180,8 +190,7 @@
     tokens, depth = activations.shape[1], activations.shape[2]
     seq_count = lengths.shape[1]
     width = depth // chunks
-    slabs = next(n for n in (2, 1) if tokens % (n * LANES) == 0 or n == 1)
-    slab = tokens // slabs
+    slabs = len(TAPER)
     tile = depth // (chunks * pairs * cores)
     kept, tail = spare_split(2 * seq_count, width)
     vmem = pl.BlockSpec(memory_space=pltpu.VMEM)
@@ -196,8 +205,8 @@
             in_specs=[anywhere] * 3,
             out_specs=[vmem] * len(offsets),
             scratch_shapes=[
-                pltpu.VMEM((count, slab, width), jnp.bfloat16),
-                pltpu.VMEM((count, slab, width), jnp.bfloat16),
+                pltpu.VMEM((len(offsets), tokens, width), jnp.bfloat16),
+                pltpu.VMEM((len(offsets), tokens, width), jnp.bfloat16),
                 pltpu.SMEM(lengths.shape, jnp.int32),
                 pltpu.SemaphoreType.DMA((count,)),
                 pltpu.SemaphoreType.DMA((count,)),
@@ -236,21 +245,34 @@
     near, far = (a.reshape(chunks, pairs, ROWS, kept) for a in (near, far))
 
     piece = width // 2 if width % (2 * LANES) == 0 else width
+    pieces = depth // piece
+    share = pl.pallas_call(
+        functools.partial(near_kernel, seq_count, kept, tail, tile),
+        out_shape=jax.ShapeDtypeStruct((pieces, 2 * tile, piece), jnp.float32),
+        in_specs=[vmem],
+        out_specs=vmem,
+        scratch_shapes=[pltpu.VMEM((pairs * ROWS, width), jnp.float32)],
+        compiler_params=pltpu.CompilerParams(vmem_limit_bytes=16 * MIB),
+        cost_estimate=pl.CostEstimate(
+            flops=4 * tile * depth * pairs * ROWS, bytes_accessed=8 * tile * depth, transcendentals=0
+        ),
+        name="near_share",
+    )(near)
     return pl.pallas_call(
-        functools.partial(factor_kernel, seq_count, seq_count * pairs * cores, kept, tail),
+        functools.partial(far_kernel, seq_count, seq_count * pairs * cores, kept, tail),
         out_shape=[jax.ShapeDtypeStruct((tile, depth), jnp.float32)] * 2,
         in_specs=[vmem] * 2,
         out_specs=[anywhere] * 2,
         scratch_shapes=[
-            pltpu.VMEM((2 * pairs * ROWS, width), jnp.float32),
-            pltpu.VMEM((depth // piece, tile, piece), jnp.float32),
-            pltpu.VMEM((depth // piece, tile, piece), jnp.float32),
-            pltpu.SemaphoreType.DMA((depth // piece,)),
-            pltpu.SemaphoreType.DMA((depth // piece,)),
+            pltpu.VMEM((pairs * ROWS, width), jnp.float32),
+            pltpu.VMEM((pieces, tile, piece), jnp.float32),
+            pltpu.VMEM((pieces, tile, piece), jnp.float32),
+            pltpu.SemaphoreType.DMA((pieces,)),
+            pltpu.SemaphoreType.DMA((pieces,)),
         ],
         compiler_params=pltpu.CompilerParams(vmem_limit_bytes=20 * MIB),
         name="factor_tiles",
-    )(near, far)
+    )(far, share)
 
 
 def solution(mesh):

time: 28.4 us -> 28.3 us (level)
  waiting for transfers between devices: 3 us -> 2.29 us
  Pallas kernels: 8.64 us -> 9.26 us
    ppermute x1, waiting for transfers between devices: 1.44 us -> 0.66 us  [local(): lax.ppermute(near, 'core', [(i, (i + 1) % cores) for i in range(cores)])]
    pallas_call x1 -> x2, Pallas kernels: 2.43 us -> 3.18 us  [the longest x1 2.4 us: local(): pl.pallas_call(functools.partial(far_kernel, seq_count, seq_count * pairs...]
  transfers between devices with their start and end apart: 4 -> 4, of which waited for: 3 -> 3; matrix products, arithmetic and copies ran while one was open for 0% -> 0% of each run, Pallas kernels for 8% -> 10%
where the time goes in v4:
time: 28.3 us; the launch traced here: 28.1 us
  blocking collectives  11.3 us (40%)
  Pallas kernels  9.26 us (33%)
  starting transfers between devices  4.63 us (16%)
  waiting for transfers between devices  2.29 us (8%)
  between operations  0.66 us (2%)
    all_to_all x1, blocking collectives, local(): lax.all_to_all(spread, ('seq', 'pair', 'core'), 0, 0, axis_index_groups=m...  11.3 us
    pallas_call x2, Pallas kernels, segment_sums(): pl.pallas_call(functools.partial(segment_kernel, seq_count, chunks, offse...  6.06 us
    ppermute x3, starting transfers between devices, local(): arrived.append(lax.ppermute(part, 'seq', ring))  4.63 us
    pallas_call x1, Pallas kernels, local(): pl.pallas_call(functools.partial(far_kernel, seq_count, seq_count * pairs...  2.4 us
    ppermute x3, waiting for transfers between devices, local(): arrived.append(lax.ppermute(part, 'seq', ring))  1.63 us
    pallas_call x1, Pallas kernels, local(): pl.pallas_call(functools.partial(near_kernel, seq_count, kept, tail, tile...  0.78 us
    ppermute x1, waiting for transfers between devices, local(): lax.ppermute(near, 'core', [(i, (i + 1) % cores) for i in range(cores)])  0.66 us
  transfers between devices with their start and end apart: 4, of which 3 were waited for; matrix products, arithmetic and copies ran while one was open for 0% of the time, Pallas kernels for 10%

profile of v4, /device:TPU:0, one launch (start us, length us, event | category | flops | bytes accessed | tf_op | source)
XLA Modules:
  0.0 28.1 jit_solution(8765846975482984881)
XLA Ops:
  0.6 4.0 %segment_sums.2 = (f32[8,768]{1,0:T(8,128)S(1)}, f32[8,768]{1,0:T(8,128)S(1)}, f32[8,768]{1,0:T(8,128)S(1)}) custom-call(bf16[1,768,4096]{2,1,0:T(8,128)(2,1)} %act.3, bf16[1,768,4096]{2,1,0:T(8,128)(2,1)} %grad.3, s32[1,3]{1,0:T(1,128)} %lens.3), custom_call_target="tpu_custom_call" | custom-call | flops 75497472 | bytes 9437184 | tf_op jit(solution)/shard_map/segment_sums/pallas_call | solution.py:202
  4.7 4.0 %collective-permute-start = (f32[8,768]{1,0:T(8,128)S(1)}, f32[8,768]{1,0:T(8,128)S(1)}, u32[]{:S(2)}, u32[]{:S(2)}) collective-permute-start(f32[8,768]{1,0:T(8,128)S(1)} %get-tuple-element.5), channel_id=1, source_target_pairs={{0,24},{8,16},{16,8},{24,0},{1,25},{9,17},{17,9},{25,1},{2,26},{10... | collective-permute-start | bytes 73736 | tf_op jit(solution)/shard_map/ppermute | solution.py:229
  8.6 0.5 %collective-permute-start.1 = (f32[8,768]{1,0:T(8,128)S(1)}, f32[8,768]{1,0:T(8,128)S(1)}, u32[]{:S(2)}, u32[]{:S(2)}) collective-permute-start(f32[8,768]{1,0:T(8,128)S(1)} %get-tuple-element.6), channel_id=1, source_target_pairs={{0,16},{8,24},{16,0},{24,8},{1,17},{9,25},{17,1},{25,9},{2,18},{10... | collective-permute-start | bytes 73736 | tf_op jit(solution)/shard_map/ppermute | solution.py:229
  9.2 0.1 collective-permute-start.2
  9.3 2.0 %segment_sums.3.refs_3_ = f32[8,768]{1,0:T(8,128)S(1)} custom-call(bf16[1,768,4096]{2,1,0:T(8,128)(2,1)} %act.3, bf16[1,768,4096]{2,1,0:T(8,128)(2,1)} %grad.3, s32[1,3]{1,0:T(1,128)} %lens.3), custom_call_target="tpu_custom_call" | custom-call | flops 25165824 | bytes 3145728 | tf_op jit(solution)/shard_map/segment_sums/pallas_call | solution.py:202
  11.3 0.0 collective-permute-done.refs_0_
  11.3 1.1 %collective-permute-done.1.refs_1_ = f32[8,768]{1,0:T(8,128)S(1)} collective-permute-done((f32[8,768]{1,0:T(8,128)S(1)}, f32[8,768]{1,0:T(8,128)S(1)}, u32[]{:S(2)}, u32[]{:S(2)}) %collective-permute-start.1) | collective-permute-done | bytes 24608 | tf_op jit(solution)/shard_map/ppermute | solution.py:229
  12.5 0.5 %collective-permute-done.2.refs_2_ = f32[8,768]{1,0:T(8,128)S(1)} collective-permute-done((f32[8,768]{1,0:T(8,128)S(1)}, f32[8,768]{1,0:T(8,128)S(1)}, u32[]{:S(2)}, u32[]{:S(2)}) %collective-permute-start.2) | collective-permute-done | bytes 24608 | tf_op jit(solution)/shard_map/ppermute | solution.py:229
  13.0 11.3 %all_to_all.5 = bf16[16,8,768]{2,1,0:T(8,128)(2,1)S(1)} all-to-all(bf16[16,8,768]{2,1,0:T(8,128)(2,1)S(1)} %mean_rows.1), channel_id=1, replica_groups={{30,26,28,24,22,18,20,16,14,10,12,8,6,2,4,0},{31,27,29,25,23,19,21,17,1..., dimensions={0} | all-to-all | bytes 393216 | tf_op jit(solution)/shard_map/all_to_all | solution.py:243
  24.3 0.0 collective-permute-start.3
  24.3 0.8 %near_share.1.share = f32[8,256,512]{2,1,0:T(8,128)S(1)} custom-call(bf16[4,4,8,768]{3,2,1,0:T(8,128)(2,1)S(1)} %bitcast.2), custom_call_target="tpu_custom_call" | custom-call | flops 67108864 | bytes 4194304 | tf_op jit(solution)/shard_map/near_share/pallas_call | solution.py:249
  25.0 0.7 %collective-permute-done.3 = bf16[16,8,768]{2,1,0:T(8,128)(2,1)S(1)} collective-permute-done((bf16[16,8,768]{2,1,0:T(8,128)(2,1)S(1)}, bf16[16,8,768]{2,1,0:T(8,128)(2,1)S(1)}, u32[]{:S(2)}, u32[]{:S(2)}) %collective-permute-start.3) | collective-permute-done | bytes 196640 | tf_op jit(solution)/shard_map/ppermute | solution.py:244
  25.7 2.4 %factor_tiles.1 = (f32[128,4096]{1,0:T(8,128)}, f32[128,4096]{1,0:T(8,128)}) custom-call(bf16[4,4,8,768]{3,2,1,0:T(8,128)(2,1)S(1)} %bitcast.3, f32[8,256,512]{2,1,0:T(8,128)S(1)} %near_share.1.share), custom_call_target="tpu_custom_call" | custom-call | tf_op jit(solution)/shard_map/factor_tiles/pallas_call | solution.py:261
  (1 shorter events, 0.0 us)
Async XLA Ops:
  4.7 6.7 %collective-permute-start = (f32[8,768]{1,0:T(8,128)S(1)}, f32[8,768]{1,0:T(8,128)S(1)}, u32[]{:S(2)}, u32[]{:S(2)}) collective-permute-start(f32[8,768]{1,0:T(8,128)S(1)} %get-tuple-element.5), channel_id=1, source_target_pairs={{0,24},{8,16},{16,8},{24,0},{1,25},{9,17},{17,9},{25,1},{2,26},{10... | collective-permute-start | bytes 73736 | tf_op jit(solution)/shard_map/ppermute | solution.py:229
  8.6 3.8 %collective-permute-start.1 = (f32[8,768]{1,0:T(8,128)S(1)}, f32[8,768]{1,0:T(8,128)S(1)}, u32[]{:S(2)}, u32[]{:S(2)}) collective-permute-start(f32[8,768]{1,0:T(8,128)S(1)} %get-tuple-element.6), channel_id=1, source_target_pairs={{0,16},{8,24},{16,0},{24,8},{1,17},{9,25},{17,1},{25,9},{2,18},{10... | collective-permute-start | bytes 73736 | tf_op jit(solution)/shard_map/ppermute | solution.py:229
  9.2 3.8 %collective-permute-start.2 = (f32[8,768]{1,0:T(8,128)S(1)}, f32[8,768]{1,0:T(8,128)S(1)}, u32[]{:S(2)}, u32[]{:S(2)}) collective-permute-start(f32[8,768]{1,0:T(8,128)S(1)} %get-tuple-element.7), channel_id=1, source_target_pairs={{0,8},{8,0},{16,24},{24,16},{1,9},{9,1},{17,25},{25,17},{2,10},{10... | collective-permute-start | bytes 73736 | tf_op jit(solution)/shard_map/ppermute | solution.py:229
  24.3 1.4 %collective-permute-start.3 = (bf16[16,8,768]{2,1,0:T(8,128)(2,1)S(1)}, bf16[16,8,768]{2,1,0:T(8,128)(2,1)S(1)}, u32[]{:S(2)}, u32[]{:S(2)}) collective-permute-start(bf16[16,8,768]{2,1,0:T(8,128)(2,1)S(1)} %all_to_all.5), channel_id=1, source_target_pairs={{0,1},{1,0},{2,3},{3,2},{4,5},{5,4},{6,7},{7,6},{8,9},{9,8},{10,11... | collective-permute-start | bytes 589832 | tf_op jit(solution)/shard_map/ppermute | solution.py:244

commit v5 on v3

--- a/solution.py
+++ b/solution.py
@@ -10,6 +10,7 @@
 
 LANES = 128
 ROWS = 8
+EVEN, TAPER = (1, 1), (3, 2, 1)
 MIB = 1 << 20
 
 
@@ -22,6 +23,12 @@
     if tail % LANES:
         return width, 0
     return kept, tail
+
+
+def spans(total, last):
+    shares = TAPER if last else EVEN
+    edges = [sum(shares[:i]) * total // sum(shares) // LANES * LANES for i in range(len(shares))] + [total]
+    return [(a, b) for a, b in zip(edges, edges[1:]) if b > a]
 
 
 def partner(index, offset, count):
@@ -62,26 +69,25 @@
     outs = refs[: len(offsets)]
     act_buf, grad_buf, len_buf, act_sem, grad_sem, len_sem = refs[len(offsets) :]
     tokens = act.shape[1]
-    slab = act_buf.shape[1]
     width = kept + tail
     rows = 2 * seq_count
     me = lax.axis_index("seq")
     len_copy = pltpu.make_async_copy(lens, len_buf, len_sem)
     len_copy.start()
-    copies = []
+    copies = {}
     for slot, offset in enumerate(offsets):
         base = partner(me, offset, chunk_count) * width
         cols = pl.ds(pl.multiple_of(base, width), width)
-        for part in range(slabs):
+        for part, (first, last) in enumerate(spans(tokens, slot == len(offsets) - 1)):
             at = slot * slabs + part
-            span = pl.ds(part * slab, slab)
+            span = pl.ds(first, last - first)
             pair = (
-                pltpu.make_async_copy(act.at[0, span, cols], act_buf.at[at], act_sem.at[at]),
-                pltpu.make_async_copy(grad.at[0, span, cols], grad_buf.at[at], grad_sem.at[at]),
+                pltpu.make_async_copy(act.at[0, span, cols], act_buf.at[slot, span], act_sem.at[at]),
+                pltpu.make_async_copy(grad.at[0, span, cols], grad_buf.at[slot, span], grad_sem.at[at]),
             )
             for copy in pair:
                 copy.start()
-            copies.append(pair)
+            copies[slot, part] = pair
     len_copy.wait()
     row = lax.broadcasted_iota(jnp.int32, (ROWS, tokens), 0)
     position = lax.broadcasted_iota(jnp.int32, (ROWS, tokens), 1) + me * tokens
@@ -102,12 +108,10 @@
     grad_member = jnp.where(member & (row >= seq_count), 1.0, 0.0).astype(jnp.bfloat16)
     for slot in range(len(offsets)):
         sums = jnp.zeros((ROWS, width), jnp.float32)
-        for part in range(slabs):
-            at = slot * slabs + part
-            span = slice(part * slab, (part + 1) * slab)
-            for member, buf, copy in zip((act_member, grad_member), (act_buf, grad_buf), copies[at]):
+        for part, (first, last) in enumerate(spans(tokens, slot == len(offsets) - 1)):
+            for member, buf, copy in zip((act_member, grad_member), (act_buf, grad_buf), copies[slot, part]):
                 copy.wait()
-                sums += jnp.dot(member[:, span], buf[at], preferred_element_type=jnp.float32)
+                sums += jnp.dot(member[:, first:last], buf[slot, first:last], preferred_element_type=jnp.float32)
         outs[slot][...] = fold(sums / count, rows, kept, tail)
 
 
@@ -131,7 +135,7 @@
     def chunk(c):
         parts = []
         for ref in (near, far):
-            block = ref[chunks - 1 - c]
+            block = ref[lax.rem(c + 1, chunks)]
             flat = block.reshape(half, kept)
             if tail:
                 flat = jnp.concatenate([flat, unfold(block, rows, kept, tail).reshape(half, tail)], axis=1)
@@ -180,8 +184,7 @@
     tokens, depth = activations.shape[1], activations.shape[2]
     seq_count = lengths.shape[1]
     width = depth // chunks
-    slabs = next(n for n in (2, 1) if tokens % (n * LANES) == 0 or n == 1)
-    slab = tokens // slabs
+    slabs = len(TAPER)
     tile = depth // (chunks * pairs * cores)
     kept, tail = spare_split(2 * seq_count, width)
     vmem = pl.BlockSpec(memory_space=pltpu.VMEM)
@@ -196,8 +199,8 @@
             in_specs=[anywhere] * 3,
             out_specs=[vmem] * len(offsets),
             scratch_shapes=[
-                pltpu.VMEM((count, slab, width), jnp.bfloat16),
-                pltpu.VMEM((count, slab, width), jnp.bfloat16),
+                pltpu.VMEM((len(offsets), tokens, width), jnp.bfloat16),
+                pltpu.VMEM((len(offsets), tokens, width), jnp.bfloat16),
                 pltpu.SMEM(lengths.shape, jnp.int32),
                 pltpu.SemaphoreType.DMA((count,)),
                 pltpu.SemaphoreType.DMA((count,)),
@@ -229,8 +232,8 @@
         name="mean_rows",
     )(*arrived)
 
-    order = list(range(pairs - 1, -1, -2)) + list(range(pairs - 2, -1, -2))
-    members = [[(s * pairs + p) * cores + c for s in range(chunks - 1, -1, -1) for p in order] for c in range(cores)]
+    order = [pairs - 1] + list(range(pairs - 1))
+    members = [[(s * pairs + p) * cores + c for s in [chunks - 1] + list(range(chunks - 1)) for p in order] for c in range(cores)]
     near = lax.all_to_all(spread, ("seq", "pair", "core"), 0, 0, axis_index_groups=members, tiled=True)
     far = lax.ppermute(near, "core", [(i, (i + 1) % cores) for i in range(cores)])
     near, far = (a.reshape(chunks, pairs, ROWS, kept) for a in (near, far))

time: 28.4 us -> 28.1 us (0.989)
  transfers between devices with their start and end apart: 4 -> 4, of which waited for: 3 -> 3; matrix products, arithmetic and copies ran while one was open for 0% -> 0% of each run, Pallas kernels for 8% -> 7%
where the time goes in v5:
time: 28.1 us; the launch traced here: 27.9 us
  blocking collectives  11.1 us (40%)
  Pallas kernels  8.51 us (30%)
  starting transfers between devices  4.63 us (16%)
  waiting for transfers between devices  3.07 us (11%)
  between operations  0.66 us (2%)
    all_to_all x1, blocking collectives, local(): lax.all_to_all(spread, ('seq', 'pair', 'core'), 0, 0, axis_index_groups=m...  11.1 us
    pallas_call x2, Pallas kernels, segment_sums(): pl.pallas_call(functools.partial(segment_kernel, seq_count, chunks, offse...  6.06 us
    ppermute x3, starting transfers between devices, local(): arrived.append(lax.ppermute(part, 'seq', ring))  4.63 us
    pallas_call x1, Pallas kernels, local(): pl.pallas_call(functools.partial(factor_kernel, seq_count, seq_count * pa...  2.43 us
    ppermute x3, waiting for transfers between devices, local(): arrived.append(lax.ppermute(part, 'seq', ring))  1.63 us
    ppermute x1, waiting for transfers between devices, local(): lax.ppermute(near, 'core', [(i, (i + 1) % cores) for i in range(cores)])  1.44 us
  transfers between devices with their start and end apart: 4, of which 3 were waited for; matrix products, arithmetic and copies ran while one was open for 0% of the time, Pallas kernels for 7%

profile of v5, /device:TPU:0, one launch (start us, length us, event | category | flops | bytes accessed | tf_op | source)
XLA Modules:
  0.0 27.9 jit_solution(6570311533608684798)
XLA Ops:
  0.6 4.0 %segment_sums.2 = (f32[8,768]{1,0:T(8,128)S(1)}, f32[8,768]{1,0:T(8,128)S(1)}, f32[8,768]{1,0:T(8,128)S(1)}) custom-call(bf16[1,768,4096]{2,1,0:T(8,128)(2,1)} %act.3, bf16[1,768,4096]{2,1,0:T(8,128)(2,1)} %grad.3, s32[1,3]{1,0:T(1,128)} %lens.3), custom_call_target="tpu_custom_call" | custom-call | flops 75497472 | bytes 9437184 | tf_op jit(solution)/shard_map/segment_sums/pallas_call | solution.py:196
  4.7 4.0 %collective-permute-start = (f32[8,768]{1,0:T(8,128)S(1)}, f32[8,768]{1,0:T(8,128)S(1)}, u32[]{:S(2)}, u32[]{:S(2)}) collective-permute-start(f32[8,768]{1,0:T(8,128)S(1)} %get-tuple-element.5), channel_id=1, source_target_pairs={{0,24},{8,16},{16,8},{24,0},{1,25},{9,17},{17,9},{25,1},{2,26},{10... | collective-permute-start | bytes 73736 | tf_op jit(solution)/shard_map/ppermute | solution.py:223
  8.6 0.5 %collective-permute-start.1 = (f32[8,768]{1,0:T(8,128)S(1)}, f32[8,768]{1,0:T(8,128)S(1)}, u32[]{:S(2)}, u32[]{:S(2)}) collective-permute-start(f32[8,768]{1,0:T(8,128)S(1)} %get-tuple-element.6), channel_id=1, source_target_pairs={{0,16},{8,24},{16,0},{24,8},{1,17},{9,25},{17,1},{25,9},{2,18},{10... | collective-permute-start | bytes 73736 | tf_op jit(solution)/shard_map/ppermute | solution.py:223
  9.2 0.1 collective-permute-start.2
  9.3 2.0 %segment_sums.3.refs_3_ = f32[8,768]{1,0:T(8,128)S(1)} custom-call(bf16[1,768,4096]{2,1,0:T(8,128)(2,1)} %act.3, bf16[1,768,4096]{2,1,0:T(8,128)(2,1)} %grad.3, s32[1,3]{1,0:T(1,128)} %lens.3), custom_call_target="tpu_custom_call" | custom-call | flops 25165824 | bytes 3145728 | tf_op jit(solution)/shard_map/segment_sums/pallas_call | solution.py:196
  11.3 0.0 collective-permute-done.refs_0_
  11.3 1.1 %collective-permute-done.1.refs_1_ = f32[8,768]{1,0:T(8,128)S(1)} collective-permute-done((f32[8,768]{1,0:T(8,128)S(1)}, f32[8,768]{1,0:T(8,128)S(1)}, u32[]{:S(2)}, u32[]{:S(2)}) %collective-permute-start.1) | collective-permute-done | bytes 24608 | tf_op jit(solution)/shard_map/ppermute | solution.py:223
  12.5 0.5 %collective-permute-done.2.refs_2_ = f32[8,768]{1,0:T(8,128)S(1)} collective-permute-done((f32[8,768]{1,0:T(8,128)S(1)}, f32[8,768]{1,0:T(8,128)S(1)}, u32[]{:S(2)}, u32[]{:S(2)}) %collective-permute-start.2) | collective-permute-done | bytes 24608 | tf_op jit(solution)/shard_map/ppermute | solution.py:223
  13.0 11.1 %all_to_all.5 = bf16[16,8,768]{2,1,0:T(8,128)(2,1)S(1)} all-to-all(bf16[16,8,768]{2,1,0:T(8,128)(2,1)S(1)} %mean_rows.1), channel_id=1, replica_groups={{30,24,26,28,6,0,2,4,14,8,10,12,22,16,18,20},{31,25,27,29,7,1,3,5,15,9,..., dimensions={0} | all-to-all | bytes 393216 | tf_op jit(solution)/shard_map/all_to_all | solution.py:237
  24.1 0.0 collective-permute-start.3
  24.1 1.4 %collective-permute-done.3 = bf16[16,8,768]{2,1,0:T(8,128)(2,1)S(1)} collective-permute-done((bf16[16,8,768]{2,1,0:T(8,128)(2,1)S(1)}, bf16[16,8,768]{2,1,0:T(8,128)(2,1)S(1)}, u32[]{:S(2)}, u32[]{:S(2)}) %collective-permute-start.3) | collective-permute-done | bytes 196640 | tf_op jit(solution)/shard_map/ppermute | solution.py:238
  25.5 2.4 %factor_tiles.1 = (f32[128,4096]{1,0:T(8,128)}, f32[128,4096]{1,0:T(8,128)}) custom-call(bf16[4,4,8,768]{3,2,1,0:T(8,128)(2,1)S(1)} %bitcast.2, bf16[4,4,8,768]{3,2,1,0:T(8,128)(2,1)S(1)} %bitcast.3), custom_call_target="tpu_custom_call" | custom-call | tf_op jit(solution)/shard_map/factor_tiles/pallas_call | solution.py:242
  (1 shorter events, 0.0 us)
Async XLA Ops:
  4.7 6.7 %collective-permute-start = (f32[8,768]{1,0:T(8,128)S(1)}, f32[8,768]{1,0:T(8,128)S(1)}, u32[]{:S(2)}, u32[]{:S(2)}) collective-permute-start(f32[8,768]{1,0:T(8,128)S(1)} %get-tuple-element.5), channel_id=1, source_target_pairs={{0,24},{8,16},{16,8},{24,0},{1,25},{9,17},{17,9},{25,1},{2,26},{10... | collective-permute-start | bytes 73736 | tf_op jit(solution)/shard_map/ppermute | solution.py:223
  8.6 3.8 %collective-permute-start.1 = (f32[8,768]{1,0:T(8,128)S(1)}, f32[8,768]{1,0:T(8,128)S(1)}, u32[]{:S(2)}, u32[]{:S(2)}) collective-permute-start(f32[8,768]{1,0:T(8,128)S(1)} %get-tuple-element.6), channel_id=1, source_target_pairs={{0,16},{8,24},{16,0},{24,8},{1,17},{9,25},{17,1},{25,9},{2,18},{10... | collective-permute-start | bytes 73736 | tf_op jit(solution)/shard_map/ppermute | solution.py:223
  9.2 3.8 %collective-permute-start.2 = (f32[8,768]{1,0:T(8,128)S(1)}, f32[8,768]{1,0:T(8,128)S(1)}, u32[]{:S(2)}, u32[]{:S(2)}) collective-permute-start(f32[8,768]{1,0:T(8,128)S(1)} %get-tuple-element.7), channel_id=1, source_target_pairs={{0,8},{8,0},{16,24},{24,16},{1,9},{9,1},{17,25},{25,17},{2,10},{10... | collective-permute-start | bytes 73736 | tf_op jit(solution)/shard_map/ppermute | solution.py:223
  24.1 1.4 %collective-permute-start.3 = (bf16[16,8,768]{2,1,0:T(8,128)(2,1)S(1)}, bf16[16,8,768]{2,1,0:T(8,128)(2,1)S(1)}, u32[]{:S(2)}, u32[]{:S(2)}) collective-permute-start(bf16[16,8,768]{2,1,0:T(8,128)(2,1)S(1)} %all_to_all.5), channel_id=1, source_target_pairs={{0,1},{1,0},{2,3},{3,2},{4,5},{5,4},{6,7},{7,6},{8,9},{9,8},{10,11... | collective-permute-start | bytes 589832 | tf_op jit(solution)/shard_map/ppermute | solution.py:238

commit v6 on v5

--- a/solution.py
+++ b/solution.py
@@ -169,8 +169,8 @@
                 pltpu.make_async_copy(act_buf.at[at], act_out.at[:, cols], act_sem.at[at]),
                 pltpu.make_async_copy(grad_buf.at[at], grad_out.at[:, cols], grad_sem.at[at]),
             )
-            for copy in pair:
-                copy.start()
+            for i, copy in enumerate(pair):
+                copy.start(priority=i)
             copies.append(pair)
     for pair in copies:
         for copy in pair:

time: 28.1 us -> 28.1 us (level)
  no operation moved by 1% of the time
where the time goes in v6:
time: 28.1 us; the launch traced here: 27.9 us
  blocking collectives  11.1 us (40%)
  Pallas kernels  8.51 us (30%)
  starting transfers between devices  4.63 us (16%)
  waiting for transfers between devices  3.07 us (11%)
  between operations  0.66 us (2%)
    all_to_all x1, blocking collectives, local(): lax.all_to_all(spread, ('seq', 'pair', 'core'), 0, 0, axis_index_groups=m...  11.1 us
    pallas_call x2, Pallas kernels, segment_sums(): pl.pallas_call(functools.partial(segment_kernel, seq_count, chunks, offse...  6.06 us
    ppermute x3, starting transfers between devices, local(): arrived.append(lax.ppermute(part, 'seq', ring))  4.63 us
    pallas_call x1, Pallas kernels, local(): pl.pallas_call(functools.partial(factor_kernel, seq_count, seq_count * pa...  2.43 us
    ppermute x3, waiting for transfers between devices, local(): arrived.append(lax.ppermute(part, 'seq', ring))  1.63 us
    ppermute x1, waiting for transfers between devices, local(): lax.ppermute(near, 'core', [(i, (i + 1) % cores) for i in range(cores)])  1.44 us
  transfers between devices with their start and end apart: 4, of which 3 were waited for; matrix products, arithmetic and copies ran while one was open for 0% of the time, Pallas kernels for 7%

profile of v6, /device:TPU:0, one launch (start us, length us, event | category | flops | bytes accessed | tf_op | source)
XLA Modules:
  0.0 27.9 jit_solution(14730841578440677074)
XLA Ops:
  0.6 4.0 %segment_sums.2 = (f32[8,768]{1,0:T(8,128)S(1)}, f32[8,768]{1,0:T(8,128)S(1)}, f32[8,768]{1,0:T(8,128)S(1)}) custom-call(bf16[1,768,4096]{2,1,0:T(8,128)(2,1)} %act.3, bf16[1,768,4096]{2,1,0:T(8,128)(2,1)} %grad.3, s32[1,3]{1,0:T(1,128)} %lens.3), custom_call_target="tpu_custom_call" | custom-call | flops 75497472 | bytes 9437184 | tf_op jit(solution)/shard_map/segment_sums/pallas_call | solution.py:196
  4.7 4.0 %collective-permute-start = (f32[8,768]{1,0:T(8,128)S(1)}, f32[8,768]{1,0:T(8,128)S(1)}, u32[]{:S(2)}, u32[]{:S(2)}) collective-permute-start(f32[8,768]{1,0:T(8,128)S(1)} %get-tuple-element.5), channel_id=1, source_target_pairs={{0,24},{8,16},{16,8},{24,0},{1,25},{9,17},{17,9},{25,1},{2,26},{10... | collective-permute-start | bytes 73736 | tf_op jit(solution)/shard_map/ppermute | solution.py:223
  8.6 0.5 %collective-permute-start.1 = (f32[8,768]{1,0:T(8,128)S(1)}, f32[8,768]{1,0:T(8,128)S(1)}, u32[]{:S(2)}, u32[]{:S(2)}) collective-permute-start(f32[8,768]{1,0:T(8,128)S(1)} %get-tuple-element.6), channel_id=1, source_target_pairs={{0,16},{8,24},{16,0},{24,8},{1,17},{9,25},{17,1},{25,9},{2,18},{10... | collective-permute-start | bytes 73736 | tf_op jit(solution)/shard_map/ppermute | solution.py:223
  9.2 0.1 collective-permute-start.2
  9.3 2.0 %segment_sums.3.refs_3_ = f32[8,768]{1,0:T(8,128)S(1)} custom-call(bf16[1,768,4096]{2,1,0:T(8,128)(2,1)} %act.3, bf16[1,768,4096]{2,1,0:T(8,128)(2,1)} %grad.3, s32[1,3]{1,0:T(1,128)} %lens.3), custom_call_target="tpu_custom_call" | custom-call | flops 25165824 | bytes 3145728 | tf_op jit(solution)/shard_map/segment_sums/pallas_call | solution.py:196
  11.3 0.0 collective-permute-done.refs_0_
  11.3 1.1 %collective-permute-done.1.refs_1_ = f32[8,768]{1,0:T(8,128)S(1)} collective-permute-done((f32[8,768]{1,0:T(8,128)S(1)}, f32[8,768]{1,0:T(8,128)S(1)}, u32[]{:S(2)}, u32[]{:S(2)}) %collective-permute-start.1) | collective-permute-done | bytes 24608 | tf_op jit(solution)/shard_map/ppermute | solution.py:223
  12.5 0.5 %collective-permute-done.2.refs_2_ = f32[8,768]{1,0:T(8,128)S(1)} collective-permute-done((f32[8,768]{1,0:T(8,128)S(1)}, f32[8,768]{1,0:T(8,128)S(1)}, u32[]{:S(2)}, u32[]{:S(2)}) %collective-permute-start.2) | collective-permute-done | bytes 24608 | tf_op jit(solution)/shard_map/ppermute | solution.py:223
  13.0 11.1 %all_to_all.5 = bf16[16,8,768]{2,1,0:T(8,128)(2,1)S(1)} all-to-all(bf16[16,8,768]{2,1,0:T(8,128)(2,1)S(1)} %mean_rows.1), channel_id=1, replica_groups={{30,24,26,28,6,0,2,4,14,8,10,12,22,16,18,20},{31,25,27,29,7,1,3,5,15,9,..., dimensions={0} | all-to-all | bytes 393216 | tf_op jit(solution)/shard_map/all_to_all | solution.py:237
  24.1 0.0 collective-permute-start.3
  24.1 1.4 %collective-permute-done.3 = bf16[16,8,768]{2,1,0:T(8,128)(2,1)S(1)} collective-permute-done((bf16[16,8,768]{2,1,0:T(8,128)(2,1)S(1)}, bf16[16,8,768]{2,1,0:T(8,128)(2,1)S(1)}, u32[]{:S(2)}, u32[]{:S(2)}) %collective-permute-start.3) | collective-permute-done | bytes 196640 | tf_op jit(solution)/shard_map/ppermute | solution.py:238
  25.5 2.4 %factor_tiles.1 = (f32[128,4096]{1,0:T(8,128)}, f32[128,4096]{1,0:T(8,128)}) custom-call(bf16[4,4,8,768]{3,2,1,0:T(8,128)(2,1)S(1)} %bitcast.2, bf16[4,4,8,768]{3,2,1,0:T(8,128)(2,1)S(1)} %bitcast.3), custom_call_target="tpu_custom_call" | custom-call | tf_op jit(solution)/shard_map/factor_tiles/pallas_call | solution.py:242
  (1 shorter events, 0.0 us)
Async XLA Ops:
  4.7 6.7 %collective-permute-start = (f32[8,768]{1,0:T(8,128)S(1)}, f32[8,768]{1,0:T(8,128)S(1)}, u32[]{:S(2)}, u32[]{:S(2)}) collective-permute-start(f32[8,768]{1,0:T(8,128)S(1)} %get-tuple-element.5), channel_id=1, source_target_pairs={{0,24},{8,16},{16,8},{24,0},{1,25},{9,17},{17,9},{25,1},{2,26},{10... | collective-permute-start | bytes 73736 | tf_op jit(solution)/shard_map/ppermute | solution.py:223
  8.6 3.8 %collective-permute-start.1 = (f32[8,768]{1,0:T(8,128)S(1)}, f32[8,768]{1,0:T(8,128)S(1)}, u32[]{:S(2)}, u32[]{:S(2)}) collective-permute-start(f32[8,768]{1,0:T(8,128)S(1)} %get-tuple-element.6), channel_id=1, source_target_pairs={{0,16},{8,24},{16,0},{24,8},{1,17},{9,25},{17,1},{25,9},{2,18},{10... | collective-permute-start | bytes 73736 | tf_op jit(solution)/shard_map/ppermute | solution.py:223
  9.2 3.8 %collective-permute-start.2 = (f32[8,768]{1,0:T(8,128)S(1)}, f32[8,768]{1,0:T(8,128)S(1)}, u32[]{:S(2)}, u32[]{:S(2)}) collective-permute-start(f32[8,768]{1,0:T(8,128)S(1)} %get-tuple-element.7), channel_id=1, source_target_pairs={{0,8},{8,0},{16,24},{24,16},{1,9},{9,1},{17,25},{25,17},{2,10},{10... | collective-permute-start | bytes 73736 | tf_op jit(solution)/shard_map/ppermute | solution.py:223
  24.1 1.4 %collective-permute-start.3 = (bf16[16,8,768]{2,1,0:T(8,128)(2,1)S(1)}, bf16[16,8,768]{2,1,0:T(8,128)(2,1)S(1)}, u32[]{:S(2)}, u32[]{:S(2)}) collective-permute-start(bf16[16,8,768]{2,1,0:T(8,128)(2,1)S(1)} %all_to_all.5), channel_id=1, source_target_pairs={{0,1},{1,0},{2,3},{3,2},{4,5},{5,4},{6,7},{7,6},{8,9},{9,8},{10,11... | collective-permute-start | bytes 589832 | tf_op jit(solution)/shard_map/ppermute | solution.py:238
